TPU v7x, 32 devices: a whole 2x2x4 slice. The times are simulated.
32 devices in a mesh: band: 8 (over z, y), grid: 4 (over x, core).
Axes of the slice: x: 2, y: 2, z: 4, core: 2. Of those that a mesh axis runs over, the one named last changes fastest.
Arguments:
- bands: bfloat16 [2, 16, 128, 128, 128], P(None, 'band', 'grid'), may hold values from -6 to 6
- occupations: float32 [16], P('band'), may hold values from 0.25 to 1
- external: float32 [128, 128, 128], P('grid'), may hold values from 0 to 2
- density_in: float32 [128, 128, 128], P('grid'), may hold values from -0.2 to 1.4
- prev_density: float32 [128, 128, 128], P('grid'), may hold values from 0 to 1.2
- prev_residual: float32 [128, 128, 128], P('grid'), may hold values from -1.3 to 0.3
- hist_density: float32 [5, 128, 128, 128], P(None, 'grid'), may hold values from 0 to 1
- hist_residual: float32 [5, 128, 128, 128], P(None, 'grid'), may hold values from -0.6 to 1
Outputs:
- density: float32 [128, 128, 128], P('grid')
- residual: float32 [128, 128, 128], P('grid')
All inputs are finite; a program needn't handle non-finite values.
Results may differ from a plain program's by a relative error of at most 0.018.
The roundings to bfloat16 on the way count: a program that leaves them out, or rounds other values in their place, can miss the bound.
Values may be sent and summed in bfloat16 or wider, within the bound.
A program may use at most 192 MiB of HBM per device.

v0:
```python
import math

import jax
import jax.numpy as jnp
from jax import lax
from jax.experimental import pallas as pl
from jax.experimental.pallas import tpu as pltpu
from jax.sharding import PartitionSpec as P

NG = 128
DEPTH = 6
ITERS = 3


time_step = 0.25
energy_shift = 2.5
coupling = 1.0
mixing_weight = 0.5
ridge_share = 0.1
ridge_floor = 0.01
density_scale = 8.0
highest = lax.Precision.HIGHEST


def fourier_tables(length, frequency):
    positions = jnp.arange(length, dtype=jnp.int32)
    phase_index = positions[:, None] * frequency[None, :] % length
    angles = phase_index.astype(jnp.float32) * (2.0 * math.pi / length)
    unit_scale = 1.0 / math.sqrt(length)
    return (
        (jnp.cos(angles) * unit_scale).astype(jnp.bfloat16),
        (jnp.sin(angles) * unit_scale).astype(jnp.bfloat16),
    )


def complex_block(cosine_part, sine_part, orientation):
    sine_signed = sine_part * orientation
    upper_half = jnp.concatenate([cosine_part, sine_signed], axis=1)
    lower_half = jnp.concatenate([-sine_signed, cosine_part], axis=1)
    return jnp.concatenate([upper_half, lower_half], axis=0)


def fold(cells):
    return jnp.sum(cells.reshape(-1, 8, cells.shape[-1]), axis=0)


def gram_kernel(hist_ref, out_ref):
    @pl.when(pl.program_id(0) == 0)
    def _():
        out_ref[...] = jnp.zeros_like(out_ref)

    count = hist_ref.shape[0]
    for plane in range(hist_ref.shape[1]):
        entries = [hist_ref[j, plane] for j in range(count)]
        place = 0
        for j in range(count):
            for k in range(j + 1):
                out_ref[place] += fold(entries[j] * entries[k])
                place += 1


def kept_products(hist):
    count, planes, rows, lanes = hist.shape
    pairs = count * (count + 1) // 2
    return pl.pallas_call(
        gram_kernel,
        grid=(planes // 2,),
        in_specs=[pl.BlockSpec((count, 2, rows, lanes), lambda i: (0, i, 0, 0))],
        out_specs=pl.BlockSpec((pairs, 8, lanes), lambda i: (0, 0, 0)),
        out_shape=jax.ShapeDtypeStruct((pairs, 8, lanes), jnp.float32),
        compiler_params=pltpu.CompilerParams(dimension_semantics=("arbitrary",)),
    )(hist)


def sums_kernel(first, fresh_count, *refs):
    hist_ref = refs[0]
    fresh = refs[1 : 1 + fresh_count]
    total_ref, now_ref, before_ref, residual_ref, newest_ref, out_ref = refs[1 + fresh_count :]

    @pl.when(pl.program_id(0) == 0)
    def _():
        out_ref[...] = jnp.zeros_like(out_ref)

    for plane in range(hist_ref.shape[1]):
        residual = total_ref[plane].astype(jnp.float32) - now_ref[plane]
        newest = residual - before_ref[plane]
        residual_ref[plane] = residual
        newest_ref[plane] = newest
        entries = [hist_ref[j, plane] for j in range(first, hist_ref.shape[0])]
        entries += [ref[plane] for ref in fresh] + [newest]
        for j, entry in enumerate(entries):
            out_ref[j] += fold(entry * newest)
            out_ref[len(entries) + j] += fold(entry * residual)


def residual_sums(first, hist, fresh, total, now, before):
    count, planes, rows, lanes = hist.shape
    cell = pl.BlockSpec((2, rows, lanes), lambda i: (i, 0, 0))
    field = jax.ShapeDtypeStruct((planes, rows, lanes), jnp.float32)
    entries = count - first + len(fresh) + 1
    return pl.pallas_call(
        lambda *refs: sums_kernel(first, len(fresh), *refs),
        grid=(planes // 2,),
        in_specs=[pl.BlockSpec((count, 2, rows, lanes), lambda i: (0, i, 0, 0))]
        + [cell] * (len(fresh) + 3),
        out_specs=(cell, cell, pl.BlockSpec((2 * entries, 8, lanes), lambda i: (0, 0, 0))),
        out_shape=(field, field, jax.ShapeDtypeStruct((2 * entries, 8, lanes), jnp.float32)),
        compiler_params=pltpu.CompilerParams(dimension_semantics=("arbitrary",)),
    )(hist, *fresh, total, now, before)


def solve_kernel(kept_ref, sums_ref, coeffs_ref, next_ref):
    last = DEPTH - 1
    shape = (8, coeffs_ref.shape[1])

    def spot(j, k):
        return j * (j + 1) // 2 + k

    values = {}
    for j in range(DEPTH):
        for k in range(j + 1):
            values[j, k] = sums_ref[k] if j == last else kept_ref[spot(j, k)]
    for j in range(last):
        for k in range(j + 1):
            next_ref[spot(j, k)] = values[j + 1, k + 1]
    trace = values[0, 0]
    for j in range(1, DEPTH):
        trace = trace + values[j, j]
    ridge = trace * (ridge_share / DEPTH) + ridge_floor
    matrix = {}
    for (j, k), value in values.items():
        matrix[j, k] = jnp.full(shape, value + ridge if j == k else value, jnp.float32)
    vector = [jnp.full(shape, sums_ref[DEPTH + j], jnp.float32) for j in range(DEPTH)]
    inverse = []
    for k in range(DEPTH):
        inverse.append(1.0 / matrix[k, k])
        scaled = {j: matrix[j, k] * inverse[k] for j in range(k + 1, DEPTH)}
        for j in range(k + 1, DEPTH):
            vector[j] = vector[j] - scaled[j] * vector[k]
            for m in range(k + 1, j + 1):
                matrix[j, m] = matrix[j, m] - scaled[j] * matrix[m, k]
    for k in reversed(range(DEPTH)):
        value = vector[k]
        for j in range(k + 1, DEPTH):
            value = value - matrix[j, k] * vector[j]
        vector[k] = value * inverse[k]
    for k in range(DEPTH):
        coeffs_ref[pl.ds(k, 1), :] = vector[k][:1]


def solve_definite(kept, sums, lanes):
    scalars = pl.BlockSpec(memory_space=pltpu.SMEM)
    return pl.pallas_call(
        solve_kernel,
        in_specs=[scalars, scalars],
        out_specs=(pl.BlockSpec(memory_space=pltpu.VMEM), scalars),
        out_shape=(
            jax.ShapeDtypeStruct((DEPTH, lanes), jnp.float32),
            jax.ShapeDtypeStruct(kept.shape, jnp.float32),
        ),
    )(kept, sums)


def local(
    bands,
    occupations,
    external,
    density_in,
    prev_density,
    prev_residual,
    hist_density,
    hist_residual,
):
    grid_count = lax.axis_size("grid")
    band_count = lax.axis_size("band")
    slab_planes = external.shape[0]
    cells_total = NG * NG * NG
    bands_total = occupations.shape[0] * band_count
    frequency = jnp.arange(-(NG // 4), NG // 4, dtype=jnp.int32)
    kept_count = frequency.shape[0]
    inside = ((frequency >= -(NG // 4)) & (frequency < NG // 4)).astype(jnp.float32)
    cosine_part, sine_part = fourier_tables(NG, frequency)
    forward_block = complex_block(cosine_part, sine_part, -1.0)
    inverse_block = complex_block(cosine_part.T, sine_part.T, 1.0)
    forward_axis = forward_block.reshape(2, NG, 2, kept_count)
    inverse_axis = inverse_block.reshape(2, kept_count, 2, NG)
    column_rows = kept_count // grid_count
    column_start = lax.axis_index("grid") * column_rows
    local_freq = lax.dynamic_slice_in_dim(frequency, column_start, column_rows).astype(jnp.float32)
    local_inside = lax.dynamic_slice_in_dim(inside, column_start, column_rows)
    squared = frequency.astype(jnp.float32) * frequency.astype(jnp.float32)
    quarter = NG / 4.0
    radius = (
        squared[None, :, None] + (local_freq * local_freq)[:, None, None] + squared[None, None, :]
    )
    kinetic = jnp.exp(-time_step * radius / (quarter * quarter))
    kinetic = kinetic * local_inside[:, None, None] * inside[None, :, None] * inside[None, None, :]
    gram_kept = lax.psum(
        jnp.sum(kept_products(hist_residual), axis=(1, 2)) / cells_total, "grid"
    )
    orbitals = jnp.concatenate([bands[0], bands[1]], axis=-1)
    density_now = density_in
    density_prev = prev_density
    residual_prev = prev_residual
    density_diffs = [hist_density[j] for j in range(DEPTH - 1)]
    residual_diffs = [hist_residual[j] for j in range(DEPTH - 1)]
    fresh = []
    residual = density_in
    for iteration in range(ITERS):
        factor = jnp.exp(-time_step * (external + coupling * density_now - energy_shift))
        doubled = jnp.concatenate([factor, factor], axis=-1)
        weighted = (orbitals.astype(jnp.float32) * doubled).astype(jnp.bfloat16)
        band_items = orbitals.shape[0]
        along_z = jnp.dot(weighted, forward_block, preferred_element_type=jnp.float32).astype(
            jnp.bfloat16
        )
        split_z = along_z.reshape(band_items, slab_planes, NG, 2, kept_count)
        along_y = jnp.einsum(
            "bxycz,cydk->bkxdz", split_z, forward_axis, preferred_element_type=jnp.float32
        )
        along_y = along_y.astype(jnp.bfloat16).reshape(
            band_items, kept_count, slab_planes, 2 * kept_count
        )
        exchanged = lax.all_to_all(along_y, "grid", split_axis=1, concat_axis=2, tiled=True)
        item_count = exchanged.shape[0]
        spread = exchanged.reshape(item_count, column_rows, NG, 2, kept_count)
        spectral = jnp.einsum(
            "byxcz,cxdk->bykdz", spread, forward_axis, preferred_element_type=jnp.float32
        )
        damped = (spectral * kinetic[None, :, :, None, :]).astype(jnp.bfloat16)
        spatial = jnp.einsum(
            "bykdz,dkcx->byxcz", damped, inverse_axis, preferred_element_type=jnp.float32
        )
        returned = lax.all_to_all(
            spatial.astype(jnp.bfloat16).reshape(item_count, column_rows, NG, 2 * kept_count),
            "grid",
            split_axis=2,
            concat_axis=1,
            tiled=True,
        )
        split_back = returned.reshape(band_items, kept_count, slab_planes, 2, kept_count)
        back_y = jnp.einsum(
            "bkxdz,dkcy->bxycz", split_back, inverse_axis, preferred_element_type=jnp.float32
        )
        back_y = back_y.astype(jnp.bfloat16).reshape(band_items, slab_planes, NG, 2 * kept_count)
        orbitals = jnp.dot(back_y, inverse_block, preferred_element_type=jnp.float32).astype(
            jnp.bfloat16
        )
        real_part = orbitals[..., :NG].astype(jnp.float32)
        imag_part = orbitals[..., NG:].astype(jnp.float32)
        weighted_sq = occupations[:, None, None, None] * (
            real_part * real_part + imag_part * imag_part
        )
        density_out = lax.psum(
            (jnp.sum(weighted_sq, axis=0) * (density_scale / bands_total)).astype(jnp.bfloat16),
            "band",
        )
        residual, newest, partial = residual_sums(
            iteration, hist_residual, fresh, density_out, density_now, residual_prev
        )
        fresh = fresh + [newest]
        density_diffs = density_diffs[-(DEPTH - 1) :] + [density_now - density_prev]
        residual_diffs = residual_diffs[-(DEPTH - 1) :] + [newest]
        sums = lax.psum(jnp.sum(partial, axis=(1, 2)) / cells_total, "grid")
        coeffs, gram_kept = solve_definite(gram_kept, sums, NG)
        density_next = density_now + mixing_weight * residual
        for j in range(DEPTH):
            combined = density_diffs[j] + mixing_weight * residual_diffs[j]
            density_next = density_next - coeffs[j][None, None, :] * combined
        density_prev = density_now
        residual_prev = residual
        density_now = density_next
    return (density_now, residual)


def solution(mesh):
    placed = (
        P(None, "band", "grid", None, None),
        P("band"),
        P("grid", None, None),
        P("grid", None, None),
        P("grid", None, None),
        P("grid", None, None),
        P(None, "grid", None, None),
        P(None, "grid", None, None),
    )
    return jax.shard_map(
        local,
        mesh=mesh,
        in_specs=placed,
        out_specs=(P("grid", None, None), P("grid", None, None)),
        check_vma=False,
    )
```

profile of v0, /device:TPU:0, one launch (start us, length us, event | category | flops | bytes accessed | tf_op | source)
XLA Modules:
  0.0 588.4 jit_solution(4792244395911128288)
XLA Ops:
  7.6 2.7 multiply_exponential_fusion.2
  10.7 1.8 copy-done.5
  13.1 1.8 fusion.41
  16.1 2.2 copy.137
  18.3 1.8 reshape.233
  20.0 4.2 all-to-all-start
  25.3 13.5 %all-to-all-done = bf16[2,64,32,128]{3,2,0,1:T(8,128)(2,1)S(1)} async-done(((bf16[2,64,32,128]{3,2,0,1:T(8,128)(2,1)}), bf16[2,64,32,128]{3,2,0,1:T(8,128)(2,1)S(1)}, u32[]{:S(2)}, u32[]{:S(2)}) %all-to-all-start) | async-done | bytes 1048608 | tf_op jit(solution)/shard_map/all_to_all | solution.py:224
  39.8 3.9 reshape.179
  43.7 1.8 fusion.69
  47.8 17.0 %all_to_all.90 = bf16[2,16,128,128]{3,1,0,2:T(8,128)(2,1)S(1)} all-to-all(bf16[2,16,128,128]{3,1,0,2:T(8,128)(2,1)S(1)} %copy.55), channel_id=1, replica_groups=mesh['band'=8,'grid'=4] {'grid'}, dimensions={2} | all-to-all | bytes 2097152 | tf_op jit(solution)/shard_map/all_to_all | solution.py:234
  66.2 3.9 reshape.181
  70.0 4.3 copy.59
  74.3 2.3 fusion.43
  81.4 11.1 %shard_map.96 = f32[15,8,128]{2,1,0:T(8,128)} custom-call(f32[5,32,128,128]{3,2,1,0:T(8,128)} %refs_0_.5), custom_call_target="tpu_custom_call" | custom-call | tf_op jit(solution)/shard_map/pallas_call | solution.py:65
  93.5 67.4 %all-reduce.5.cloned.1.call-done.refs_1_ = bf16[32,128,128]{2,1,0:T(8,128)(2,1)} async-done(((bf16[32,128,128]{2,1,0:T(8,128)(2,1)}), bf16[32,128,128]{2,1,0:T(8,128)(2,1)}) %all-reduce.5.cloned.1.call-update) | async-done | bytes 1048592 | tf_op jit(solution)/shard_map/psum | solution.py:254
  160.9 12.6 %shard_map.95 = (f32[32,128,128]{2,1,0:T(8,128)}, f32[32,128,128]{2,1,0:T(8,128)}, f32[12,8,128]{2,1,0:T(8,128)}) custom-call(f32[5,32,128,128]{3,2,1,0:T(8,128)} %refs_0_.5, bf16[32,128,128]{2,1,0:T(8,128)(2,1)} %all-reduce.5.cloned.1.call-done.refs_1_, f32[32,128,128]{2,1,0:T(8,128)} %refs_2_.1, f32[32,128,128]{2,1,0:T(8,128)} %refs_3_.1), custom_call_target="tpu_custom_call" | custom-call | tf_op jit(solution)/shard_map/pallas_call | solution.py:101
  174.5 7.4 %all-reduce = (f32[15]{0:T(128)}, f32[12]{0:T(128)}) all-reduce(f32[15]{0:T(128)S(1)} %broadcast_multiply_fusion.3, f32[12]{0:T(128)S(1)} %broadcast_multiply_fusion.2), channel_id=1, replica_groups=mesh['band'=8,'grid'=4] {'grid'}, use_global_device_ids=true, to_apply=%region_3.4 | all-reduce | flops 27 | bytes 216 | tf_op jit(solution)/shard_map/psum | solution.py:198
  184.2 12.6 %multiply_exponential_fusion.1 = (f32[32,128,128]{2,1,0:T(8,128)S(1)}, f32[32,128,128]{2,1,0:T(8,128)}) fusion(f32[32,128,128]{2,1,0:T(8,128)} %param.10, f32[32,128,128]{2,1,0:T(8,128)} %get-tuple-element.19.refs_1_, f32[32,128,128]{2,1,0:T(8,128)S(1)} %copy-done, f32[32,128,128]{2,1,0:T(8,128)} %param.12, f32[128]{0:T(128)S(1)} %get-tuple-element.51, ...), kind=kLoop, calls=%fused_computation.79 | loop fusion | flops 15728640 | bytes 35654656 | tf_op jit(solution)/shard_map/exp | solution.py:210
  197.2 1.8 copy-done.2
  201.9 3.5 copy.150
  205.3 4.8 reshape.234
  210.1 17.9 %all_to_all.91 = bf16[2,64,32,128]{3,2,0,1:T(8,128)(2,1)S(1)} all-to-all(bf16[2,64,32,128]{3,2,0,1:T(8,128)(2,1)} %reshape.234), channel_id=1, replica_groups=mesh['band'=8,'grid'=4] {'grid'}, dimensions={1} | all-to-all | bytes 2097152 | tf_op jit(solution)/shard_map/all_to_all | solution.py:224
  229.1 5.0 reshape.185
  234.1 3.4 fusion.70
  237.5 2.3 copy.70
  239.8 2.7 copy.71
  242.4 18.1 %all_to_all.92 = bf16[2,16,128,128]{3,1,0,2:T(8,128)(2,1)S(1)} all-to-all(bf16[2,16,128,128]{3,1,0,2:T(8,128)(2,1)} %copy.71), channel_id=1, replica_groups=mesh['band'=8,'grid'=4] {'grid'}, dimensions={2} | all-to-all | bytes 2097152 | tf_op jit(solution)/shard_map/all_to_all | solution.py:234
  261.9 5.0 reshape.187
  266.9 6.5 %copy.75 = bf16[2,64,32,2,64]{1,4,3,2,0:T(8,128)(2,1)} copy(bf16[2,64,32,2,64]{4,3,2,1,0:T(2,128)(2,1)} %reshape.187) | data formatting | bytes 2097152 | tf_op jit(solution)/shard_map/reshape | solution.py:241
  273.4 2.3 fusion.47
  280.5 76.6 %all-reduce.7.cloned.1.call-done.refs_2_ = bf16[32,128,128]{2,1,0:T(8,128)(2,1)} async-done(((bf16[32,128,128]{2,1,0:T(8,128)(2,1)}), bf16[32,128,128]{2,1,0:T(8,128)(2,1)}) %all-reduce.7.cloned.1.call-update) | async-done | bytes 1048592 | tf_op jit(solution)/shard_map/psum | solution.py:254
  357.0 13.0 %shard_map.98 = (f32[32,128,128]{2,1,0:T(8,128)}, f32[32,128,128]{2,1,0:T(8,128)}, f32[12,8,128]{2,1,0:T(8,128)}) custom-call(f32[5,32,128,128]{3,2,1,0:T(8,128)} %refs_0_.5, f32[32,128,128]{2,1,0:T(8,128)} %get-tuple-element.19.refs_1_, bf16[32,128,128]{2,1,0:T(8,128)(2,1)} %all-reduce.7.cloned.1.call-done.refs_2_, ...), custom_call_target="tpu_custom_call" | custom-call | tf_op jit(solution)/shard_map/pallas_call | solution.py:101
  371.0 7.0 %psum.53.sums_ref = f32[12]{0:T(128)} all-reduce(f32[12]{0:T(128)S(1)} %broadcast_multiply_fusion.1), channel_id=1, replica_groups=mesh['band'=8,'grid'=4] {'grid'}, use_global_device_ids=true, to_apply=%region_9.10 | all-reduce | flops 12 | bytes 96 | tf_op jit(solution)/shard_map/psum | solution.py:264
  380.3 12.6 %multiply_exponential_fusion = (f32[32,128,128]{2,1,0:T(8,128)S(1)}, f32[32,128,128]{2,1,0:T(8,128)}) fusion(f32[32,128,128]{2,1,0:T(8,128)} %param.10, f32[32,128,128]{2,1,0:T(8,128)} %get-tuple-element.24.refs_2_, f32[32,128,128]{2,1,0:T(8,128)} %get-tuple-element.35.refs_3_, f32[32,128,128]{2,1,0:T(8,128)S(1)} %copy-done, f32[128]{0:T(128)S(1)} %get-tuple-element.45, ...), kind=kLoop, calls=%fused_computation.76 | loop fusion | flops 16252928 | bytes 35654656 | tf_op jit(solution)/shard_map/exp | solution.py:210
  393.3 1.8 copy-done.4
  397.9 3.5 copy.163
  401.4 4.8 reshape.235
  406.2 17.9 %all_to_all.93 = bf16[2,64,32,128]{3,2,0,1:T(8,128)(2,1)S(1)} all-to-all(bf16[2,64,32,128]{3,2,0,1:T(8,128)(2,1)} %reshape.235), channel_id=1, replica_groups=mesh['band'=8,'grid'=4] {'grid'}, dimensions={1} | all-to-all | bytes 2097152 | tf_op jit(solution)/shard_map/all_to_all | solution.py:224
  425.2 5.0 reshape.191
  430.2 3.4 fusion.71
  436.5 18.1 %all_to_all.94 = bf16[2,16,128,128]{3,1,0,2:T(8,128)(2,1)S(1)} all-to-all(bf16[2,16,128,128]{3,1,0,2:T(8,128)(2,1)} %copy.87), channel_id=1, replica_groups=mesh['band'=8,'grid'=4] {'grid'}, dimensions={2} | all-to-all | bytes 2097152 | tf_op jit(solution)/shard_map/all_to_all | solution.py:234
  455.1 1.8 reshape.193
  456.9 6.5 %copy.91 = bf16[2,64,32,2,64]{1,4,3,2,0:T(8,128)(2,1)} copy(bf16[2,64,32,2,64]{4,3,2,1,0:T(2,128)(2,1)} %reshape.193) | data formatting | bytes 2097152 | tf_op jit(solution)/shard_map/reshape | solution.py:241
  463.4 2.3 fusion.51
  469.5 76.6 %all-reduce.9.cloned.1.call-done.refs_3_ = bf16[32,128,128]{2,1,0:T(8,128)(2,1)} async-done(((bf16[32,128,128]{2,1,0:T(8,128)(2,1)}), bf16[32,128,128]{2,1,0:T(8,128)(2,1)}) %all-reduce.9.cloned.1.call-update) | async-done | bytes 1048592 | tf_op jit(solution)/shard_map/psum | solution.py:254
  546.1 13.3 %shard_map.100 = (f32[32,128,128]{2,1,0:T(8,128)}, f32[32,128,128]{2,1,0:T(8,128)}, f32[12,8,128]{2,1,0:T(8,128)}) custom-call(f32[5,32,128,128]{3,2,1,0:T(8,128)} %refs_0_.5, f32[32,128,128]{2,1,0:T(8,128)} %get-tuple-element.19.refs_1_, f32[32,128,128]{2,1,0:T(8,128)} %get-tuple-element.24.refs_2_, ...), custom_call_target="tpu_custom_call" | custom-call | tf_op jit(solution)/shard_map/pallas_call | solution.py:101
  560.4 7.0 %psum.55.sums_ref = f32[12]{0:T(128)} all-reduce(f32[12]{0:T(128)S(1)} %broadcast_multiply_fusion), channel_id=1, replica_groups=mesh['band'=8,'grid'=4] {'grid'}, use_global_device_ids=true, to_apply=%region_13.14 | all-reduce | flops 12 | bytes 96 | tf_op jit(solution)/shard_map/psum | solution.py:264
  569.7 11.9 %fusion.26 = f32[32,128,128]{2,1,0:T(8,128)} fusion(f32[32,128,128]{2,1,0:T(8,128)} %get-tuple-element.29, f32[32,128,128]{2,1,0:T(8,128)} %get-tuple-element.33.refs_4_, f32[32,128,128]{2,1,0:T(8,128)} %get-tuple-element.35.refs_3_, f32[32,128,128]{2,1,0:T(8,128)} %get-tuple-element.15, f32[128]{0:T(128)S(1)} %get-tuple-element.39, ...), kind=kLoop, calls=%fused_computation.52 | loop fusion | flops 15204352 | bytes 31460352 | tf_op jit(solution)/shard_map/sub | solution.py:269
  (77 shorter events, 45.5 us)
Async XLA Ops:
  10.3 2.2 copy-start.5
  20.0 18.7 %all-to-all-start = ((bf16[2,64,32,128]{3,2,0,1:T(8,128)(2,1)}), bf16[2,64,32,128]{3,2,0,1:T(8,128)(2,1)S(1)}, u32[]{:S(2)}, u32[]{:S(2)}) async-start(bf16[2,64,32,128]{3,2,0,1:T(8,128)(2,1)} %reshape.233), calls=%async_computation | async-start | bytes 2097152 | tf_op jit(solution)/shard_map/all_to_all | solution.py:224
  24.3 136.7 %all-reduce.5.cloned.1.call-start = ((), (), s32[]{:S(2)}) async-start(), calls=%async_computation.6 | async-start | bytes 2097152 | tf_op jit(solution)/shard_map/psum | solution.py:254
  76.9 1.3 copy-start.6
  78.2 1.9 copy-start.1
  81.4 275.7 %all-reduce.7.cloned.1.call-start = ((), (), s32[]{:S(2)}) async-start(), calls=%async_computation.7 | async-start | bytes 2097152 | tf_op jit(solution)/shard_map/psum | solution.py:254
  93.5 90.7 %copy-start = (f32[32,128,128]{2,1,0:T(8,128)S(1)}, f32[32,128,128]{2,1,0:T(8,128)}, u32[]{:S(2)}) copy-start(f32[32,128,128]{2,1,0:T(8,128)} %refs_2_.1) | copy-start | bytes 6291460
  196.9 2.2 copy-start.2
  277.3 1.9 copy-start.3
  280.4 265.7 %all-reduce.9.cloned.1.call-start = ((), (), s32[]{:S(2)}) async-start(), calls=%async_computation.8 | async-start | bytes 2097152 | tf_op jit(solution)/shard_map/psum | solution.py:254
  392.9 2.2 copy-start.4
Sparse Core Ops, SparseCore 0:
  81.5 79.3 all-reduce.4
  280.6 76.4 all-reduce.6
  469.6 76.4 all-reduce.8
where the time goes:
time: 598 us; the launch traced here: 588 us
  waiting for transfers between devices  234 us (39%)
  blocking collectives  110 us (18%)
  local copies, waits for them, and re-layouts  90.4 us (15%)
  Pallas kernels  54 us (9%)
  other arithmetic  52.7 us (9%)
  matrix products  28 us (5%)
  between operations  14.4 us (2%)
    psum x3, waiting for transfers between devices, local(): lax.psum((jnp.sum(weighted_sq, axis=0) * (density_scale / bands_total)).a...  221 us
    all_to_all x3, blocking collectives, local(): lax.all_to_all(spatial.astype(jnp.bfloat16).reshape(item_count, column_ro...  53.2 us
    pallas_call x3, Pallas kernels, residual_sums(): pl.pallas_call(lambda *refs: sums_kernel(first, len(fresh), *refs), grid=...  38.8 us
    all_to_all x2, blocking collectives, local(): lax.all_to_all(along_y, 'grid', split_axis=1, concat_axis=2, tiled=True)  35.8 us
    reshape x6, local copies, waits for them, and re-layouts, local(): returned.reshape(band_items, kept_count, slab_planes, 2, kept_count)  28 us
    exp x3, other arithmetic, local(): jnp.exp(-time_step * (external + coupling * density_now - energy_shift))  28 us
    reshape x6, local copies, waits for them, and re-layouts, local(): along_y.astype(jnp.bfloat16)  20.4 us
    psum x2, blocking collectives, local(): sums = lax.psum(jnp.sum(partial, axis=(1, 2)) / cells_total, 'grid')  14 us
  transfers between devices with their start and end apart: 4, of which 4 were waited for; matrix products, arithmetic and copies ran while one was open for 0% of the time, Pallas kernels for 2%

commit v1 on v0

v1 whole, which is shorter than its diff:
```python
import functools
import math

import jax
import jax.numpy as jnp
import numpy as np
from jax import lax
from jax.experimental import pallas as pl
from jax.experimental.pallas import tpu as pltpu
from jax.sharding import PartitionSpec as P

DEPTH = 6
ITERS = 3

time_step = 0.25
energy_shift = 2.5
coupling = 1.0
mixing_weight = 0.5
ridge_share = 0.1
ridge_floor = 0.01
density_scale = 8.0

MESH = pl.DeviceIdType.MESH
BF = jnp.bfloat16
F32 = jnp.float32


def make_tables(ng):
    freq = np.arange(-(ng // 4), ng // 4)
    phase = (np.arange(ng)[:, None] * freq[None, :]) % ng
    angles = phase.astype(np.float64) * (2.0 * math.pi / ng)
    cos = (np.cos(angles) / math.sqrt(ng)).astype(np.float32)
    sin = (np.sin(angles) / math.sqrt(ng)).astype(np.float32)
    forward_z = np.concatenate(
        [np.concatenate([cos, -sin, -sin, -cos], 1), np.concatenate([sin, cos, cos, -sin], 1)], 0
    )
    forward = np.concatenate([cos.T, sin.T], 1)
    inverse = np.concatenate([cos, -sin], 1)
    inverse_z = np.concatenate(
        [np.concatenate([cos.T, sin.T], 1), np.concatenate([-sin.T, cos.T], 1)], 0
    )
    quarter = ng / 4.0
    damp = np.exp(-time_step * (freq.astype(np.float64) ** 2) / (quarter * quarter))
    damp = damp * ((freq >= -(ng // 4)) & (freq < ng // 4))
    pair = damp[:, None] * np.concatenate([damp, damp])[None, :]
    single = np.broadcast_to(damp[:, None], (damp.shape[0], 2 * damp.shape[0]))
    as_bf = lambda table: jnp.asarray(table, F32).astype(BF)
    return (
        as_bf(forward_z),
        as_bf(forward),
        as_bf(inverse),
        as_bf(inverse_z),
        jnp.asarray(pair, F32),
        jnp.asarray(np.ascontiguousarray(single), F32),
    )


def dot(a, b):
    return jnp.dot(a, b, preferred_element_type=F32)


def fold(cells):
    return jnp.sum(cells.reshape(-1, 8, cells.shape[-1]), axis=0)


def spot(j, k):
    return (j * (j + 1) // 2 + k) if j >= k else (k * (k + 1) // 2 + j)


def solve(gram, vector):
    trace = gram[0, 0]
    for j in range(1, DEPTH):
        trace = trace + gram[j, j]
    ridge = trace * (ridge_share / DEPTH) + ridge_floor
    matrix = {(j, k): gram[j, k] + ridge if j == k else gram[j, k] for (j, k) in gram}
    vector = list(vector)
    inverse = []
    for k in range(DEPTH):
        inverse.append(1.0 / matrix[k, k])
        scaled = {j: matrix[j, k] * inverse[k] for j in range(k + 1, DEPTH)}
        for j in range(k + 1, DEPTH):
            vector[j] = vector[j] - scaled[j] * vector[k]
            for m in range(k + 1, j + 1):
                matrix[j, m] = matrix[j, m] - scaled[j] * matrix[m, k]
    for k in reversed(range(DEPTH)):
        value = vector[k]
        for j in range(k + 1, DEPTH):
            value = value - matrix[j, k] * vector[j]
        vector[k] = value * inverse[k]
    return vector


def kernel(
    dims,
    occ_in,
    bands,
    external,
    density_in,
    prev_density,
    prev_residual,
    hist_density,
    hist_residual,
    fz,
    fy,
    iy,
    iz,
    pair_damp,
    single_damp,
    density_out,
    residual_out,
    psi,
    send_f,
    recv_f,
    send_b,
    recv_b,
    xscr,
    dscr,
    fac,
    ext,
    rho0,
    q_hist,
    t_hist,
    now,
    res,
    prev,
    parts,
    sums,
    gsc,
    occ,
    gath,
    staged,
    load_sem,
    f1_send,
    f1_recv,
    f_send,
    f_recv,
    b_send,
    b_recv,
    e_send,
    e_recv,
    a_send,
    a_recv,
    o_send,
    o_recv,
    g_send,
    g_recv,
    out_sem,
):
    G, M, H, NB, PL, C, K, PB, NG = dims
    kept = C * G
    peers = G * M
    xs = C + 8
    ds = NG + 8
    g = lax.axis_index("grid")
    b = lax.axis_index("band")
    m = lax.rem(b, M)
    h = b // M
    rank = m * G + g

    def place(r):
        other = lax.rem(rank + r, peers)
        return other // G, lax.rem(other, G)

    def source(r):
        other = lax.rem(rank + peers - r, peers)
        return other // G, lax.rem(other, G)

    def device(mm, gg):
        return (h * M + mm, gg)

    loads = []

    def load(src, dst):
        copy = pltpu.make_async_copy(src, dst, load_sem.at[len(loads)])
        copy.start()
        loads.append(copy)
        return copy

    first = [load(external, ext), load(density_in, rho0)]
    for t in range(NB):
        for j in range(M):
            for c in range(2):
                first.append(load(bands.at[c, t, pl.ds(j * PL, PL)], psi.at[t, j, c]))
    mine = pl.ds(m * PL, PL)
    later = [
        load(density_in.at[mine], now.at[0]),
        load(prev_density.at[mine], prev),
        load(prev_residual.at[mine], res.at[0]),
    ]
    for j in range(DEPTH - 1):
        later.append(load(hist_residual.at[j, mine], q_hist.at[j]))
        later.append(load(hist_density.at[j, mine], t_hist.at[j]))

    barrier = pltpu.get_barrier_semaphore()

    def greet(r, _):
        mm, gg = place(r)
        pl.semaphore_signal(barrier, inc=1, device_id=device(mm, gg), device_id_type=MESH)
        return 0

    lax.fori_loop(1, peers, greet, 0)

    def greet_half(r, _):
        hh = lax.rem(h + r, H)
        pl.semaphore_signal(barrier, inc=1, device_id=(hh * M + m, g), device_id_type=MESH)
        return 0

    lax.fori_loop(1, H, greet_half, 0)

    lane = lax.broadcasted_iota(jnp.int32, (1, NG), 1)
    sign = jnp.where(lane < NG // 2, 1.0, -1.0).astype(F32)

    def rot(x):
        return pltpu.roll(x, NG // 2, 1) * sign

    def f1_copy(t, r):
        gg = lax.rem(g + r, G)
        return pltpu.make_async_remote_copy(
            src_ref=send_f.at[t, gg],
            dst_ref=recv_f.at[t, g],
            send_sem=f1_send.at[t, r],
            recv_sem=f1_recv.at[t, r],
            device_id=(b, gg),
            device_id_type=MESH,
        )

    def f_copy(t, r):
        mm, gg = place(r)
        return pltpu.make_async_remote_copy(
            src_ref=send_f.at[t, gg, mm],
            dst_ref=recv_f.at[t, g, m],
            send_sem=f_send.at[t, r],
            recv_sem=f_recv.at[t, r],
            device_id=device(mm, gg),
            device_id_type=MESH,
        )

    def b_copy(k, r):
        mm, gg = place(r)
        return pltpu.make_async_remote_copy(
            src_ref=send_b.at[k, gg, mm],
            dst_ref=recv_b.at[k, m, g],
            send_sem=b_send.at[k, r],
            recv_sem=b_recv.at[k, r],
            device_id=device(mm, gg),
            device_id_type=MESH,
        )

    def e_copy(it, k, r):
        hh = lax.rem(h + r, H)
        rows = pl.ds(k * PB, PB)
        return pltpu.make_async_remote_copy(
            src_ref=parts.at[it, h, rows],
            dst_ref=parts.at[it, h, rows],
            send_sem=e_send.at[it, k, r],
            recv_sem=e_recv.at[it, k, r],
            device_id=(hh * M + m, g),
            device_id_type=MESH,
        )

    def a_copy(it, r):
        mm, gg = place(r)
        return pltpu.make_async_remote_copy(
            src_ref=sums.at[it, rank],
            dst_ref=sums.at[it, rank],
            send_sem=a_send.at[r],
            recv_sem=a_recv.at[r],
            device_id=device(mm, gg),
            device_id_type=MESH,
        )

    def o_copy(r):
        mm = lax.rem(m + r, M)
        return pltpu.make_async_remote_copy(
            src_ref=occ.at[m],
            dst_ref=occ.at[m],
            send_sem=o_send.at[r],
            recv_sem=o_recv.at[r],
            device_id=device(mm, g),
            device_id_type=MESH,
        )

    def g_copy(which, r):
        mm = lax.rem(m + r, M)
        return pltpu.make_async_remote_copy(
            src_ref=gath.at[which, m],
            dst_ref=gath.at[which, m],
            send_sem=g_send.at[which, r],
            recv_sem=g_recv.at[which, r],
            device_id=device(mm, g),
            device_id_type=MESH,
        )

    def start_all(make, count):
        def body(r, _):
            make(r).start()
            return 0

        lax.fori_loop(1, count, body, 0)

    def wait_sent(make, count):
        def body(r, _):
            make(r).wait_send()
            return 0

        lax.fori_loop(1, count, body, 0)

    def wait_arrived(make, count):
        def body(r, _):
            make(r).wait_recv()
            return 0

        lax.fori_loop(1, count, body, 0)

    def forward_zy(t, per_block):
        def body(j, _):
            place_of = j if per_block else 0
            for two in range(PL // 2):
                rows = []
                for q in (2 * two, 2 * two + 1):
                    f = fac[place_of, q]
                    real = (psi[t, j, 0, q].astype(F32) * f).astype(BF)
                    imag = (psi[t, j, 1, q].astype(F32) * f).astype(BF)
                    rows.append(jnp.concatenate([real, imag], axis=1))
                along = dot(jnp.concatenate(rows, axis=0), fz[...]).astype(BF)
                top = jnp.concatenate([along[:NG, :NG], along[NG:, :NG]], axis=1)
                low = jnp.concatenate([along[:NG, NG:], along[NG:, NG:]], axis=1)
                out = dot(fy[...], jnp.concatenate([top, low], axis=0)).astype(BF)
                for side in range(2):
                    for gg in range(G):
                        send_f[t, gg, j, 2 * two + side] = out[
                            gg * C : (gg + 1) * C, side * NG : (side + 1) * NG
                        ]
            return 0

        lax.fori_loop(0, M, body, 0)

    def spectral(t):
        def spread(blk, _):
            gg, mm = blk // M, lax.rem(blk, M)
            for p in range(PL):
                start = pl.multiple_of((blk * PL + p) * xs, 8)
                xscr[pl.ds(start, C), :] = recv_f[t, gg, mm, p].astype(F32)
            return 0

        lax.fori_loop(0, peers, spread, 0)
        unroll = min(4, C)

        def columns(part, _):
            for two in range(unroll // 2):
                stacked = []
                for side in range(2):
                    kl = part * unroll + two * 2 + side
                    x = xscr[pl.ds(kl, NG, stride=xs), :]
                    stacked.append(jnp.concatenate([x.astype(BF), rot(x).astype(BF)], axis=0))
                c = dot(fy[...], jnp.concatenate(stacked, axis=1))
                stacked = []
                for side in range(2):
                    kl = part * unroll + two * 2 + side
                    damp = pair_damp[...] * single_damp[pl.ds(g * C + kl, 1), :]
                    one = c[:, side * NG : (side + 1) * NG] * damp
                    stacked.append(jnp.concatenate([one.astype(BF), rot(one).astype(BF)], axis=0))
                d = dot(iy[...], jnp.concatenate(stacked, axis=1))
                for side in range(2):
                    kl = part * unroll + two * 2 + side
                    start = pl.multiple_of(kl * ds, 8)
                    dscr[pl.ds(start, NG), :] = d[:, side * NG : (side + 1) * NG]
            return 0

        lax.fori_loop(0, C // unroll, columns, 0)

        def collect(blk, _):
            gg, mm = blk // M, lax.rem(blk, M)
            for p in range(PL):
                v = dscr[pl.ds(blk * PL + p, C, stride=ds), :]
                send_b[p // PB, gg, mm, p % PB, t] = v.astype(BF)
            return 0

        lax.fori_loop(0, peers, collect, 0)

    def inverse_yz(it, k):
        keep = it < ITERS - 1

        def body(pp, _):
            p = k * PB + pp
            total = jnp.zeros((NG, NG), F32)
            for j in range(M):
                stacked = []
                for t in range(NB):
                    d = jnp.concatenate(
                        [recv_b[k, j, gg, pp, t].astype(F32) for gg in range(G)], axis=0
                    )
                    stacked.append(jnp.concatenate([d.astype(BF), rot(d).astype(BF)], axis=0))
                e = dot(iy[...], jnp.concatenate(stacked, axis=1)).astype(BF)
                e = jnp.concatenate([e[:, t * NG : (t + 1) * NG] for t in range(NB)], axis=0)
                wave = dot(e, iz[...]).astype(BF)
                for t in range(NB):
                    real = wave[t * NG : (t + 1) * NG, :NG]
                    imag = wave[t * NG : (t + 1) * NG, NG:]
                    if keep:
                        psi[t, j, 0, p] = real
                        psi[t, j, 1, p] = imag
                    real = real.astype(F32)
                    imag = imag.astype(F32)
                    total = total + occ[j, t] * (real * real + imag * imag)
            parts[it, h, p] = (total * (density_scale / (NB * M * H))).astype(BF)
            return 0

        lax.fori_loop(0, PB, body, 0)

    for t in range(NB):
        occ[m, t] = jnp.full((1, NG), occ_in[t], F32)

    for copy in first:
        copy.wait()

    def first_factor(j, _):
        for q in range(PL):
            plane = j * PL + q
            fac[j, q] = jnp.exp(-time_step * (ext[plane] + coupling * rho0[plane] - energy_shift))
        return 0

    lax.fori_loop(0, M, first_factor, 0)

    cells = 1.0 / (NG * NG * NG)
    for it in range(ITERS):
        slot = (DEPTH - 1 + it) % DEPTH
        forward_make = f1_copy if it == 0 else f_copy
        forward_count = G if it == 0 else peers
        for t in range(NB):
            if it > 0:
                wait_sent(functools.partial(f1_copy if it == 1 else f_copy, t), G if it == 1 else peers)
            forward_zy(t, it == 0)
            if it == 0 and t == 0:
                pl.semaphore_wait(barrier, peers - 1 + H - 1)
                start_all(o_copy, M)
            start_all(functools.partial(forward_make, t), forward_count)
            if it == 0:
                recv_f[t, g] = send_f[t, g]
            else:
                recv_f[t, g, m] = send_f[t, g, m]
        if it == 0:
            for copy in later:
                copy.wait()

            def prepare(p, accs):
                entries = [q_hist[j, p] for j in range(DEPTH - 1)]
                out = list(accs)
                for j in range(DEPTH - 1):
                    t_hist[j, p] = t_hist[j, p] + mixing_weight * entries[j]
                    for kk in range(j + 1):
                        out[spot(j, kk)] = out[spot(j, kk)] + fold(entries[j] * entries[kk])
                return tuple(out)

            zeros = tuple(jnp.zeros((8, NG), F32) for _ in range(spot(DEPTH - 1, 0)))
            kept_sums = lax.fori_loop(0, PL, prepare, zeros)
            line = jnp.zeros((1, NG), F32)
            for n, acc in enumerate(kept_sums):
                value = jnp.sum(jnp.sum(acc, axis=0, keepdims=True), axis=1, keepdims=True)
                line = line + jnp.where(lane == 2 * DEPTH + n, value, 0.0)
            gsc[0] = line
        for t in range(NB):
            wait_arrived(functools.partial(forward_make, t), forward_count)
            if it > 0 and t == 0:
                for k in range(K):
                    wait_sent(functools.partial(b_copy, k), peers)
            spectral(t)
        for k in range(K):
            start_all(functools.partial(b_copy, k), peers)
            recv_b[k, m, g] = send_b[k, g, m]
        if it == 0:
            wait_arrived(o_copy, M)
        for k in range(K):
            wait_arrived(functools.partial(b_copy, k), peers)
            inverse_yz(it, k)
            start_all(functools.partial(e_copy, it, k), H)

        accs = tuple(jnp.zeros((8, NG), F32) for _ in range(2 * DEPTH))
        for k in range(K):
            wait_arrived(functools.partial(e_copy, it, k), H)

            def gather_sums(p, accs, it=it, slot=slot):
                rho = parts[it, 0, p].astype(F32)
                for hh in range(1, H):
                    rho = rho + parts[it, hh, p].astype(F32)
                before = prev[p] if it == 0 else now[it - 1, p]
                here = now[it, p]
                residual = rho - here
                newest = residual - res[it, p]
                res[it + 1, p] = residual
                q_hist[slot, p] = newest
                t_hist[slot, p] = (here - before) + mixing_weight * newest
                out = list(accs)
                for j in range(DEPTH):
                    entry = newest if j == slot else q_hist[j, p]
                    out[j] = out[j] + fold(entry * newest)
                    out[DEPTH + j] = out[DEPTH + j] + fold(entry * residual)
                if it == ITERS - 1:
                    gath[1, m, p] = residual.astype(BF)
                return tuple(out)

            accs = lax.fori_loop(k * PB, (k + 1) * PB, gather_sums, accs)
        if it == ITERS - 1:
            start_all(functools.partial(g_copy, 1), M)
        line = gsc[0] if it == 0 else jnp.zeros((1, NG), F32)
        for n, acc in enumerate(accs):
            value = jnp.sum(jnp.sum(acc, axis=0, keepdims=True), axis=1, keepdims=True)
            line = line + jnp.where(lane == n, value, 0.0)
        if it > 0:
            wait_sent(functools.partial(a_copy, it - 1), peers)
        sums[it, rank] = line
        start_all(functools.partial(a_copy, it), peers)
        wait_arrived(functools.partial(a_copy, it), peers)
        total = sums[it, 0]
        for r in range(1, peers):
            total = total + sums[it, r]
        total = total * cells

        def pick(n):
            value = jnp.sum(jnp.where(lane == n, total, 0.0), axis=1, keepdims=True)
            return jnp.broadcast_to(value, (1, NG))

        if it == 0:
            for n in range(spot(DEPTH - 1, 0)):
                gsc[1 + n] = pick(2 * DEPTH + n)
        vector = [pick(DEPTH + j) for j in range(DEPTH)]
        for j in range(DEPTH):
            gsc[1 + spot(j, slot)] = pick(j)
        gram = {(j, kk): gsc[1 + spot(j, kk)] for j in range(DEPTH) for kk in range(j + 1)}
        coeffs = solve(gram, vector)

        def mix(p, _, it=it, coeffs=coeffs):
            value = now[it, p] + mixing_weight * res[it + 1, p]
            for j in range(DEPTH):
                value = value - coeffs[j] * t_hist[j, p]
            if it == ITERS - 1:
                gath[0, m, p] = value.astype(BF)
            else:
                now[it + 1, p] = value
                own = ext[m * PL + p]
                fac[0, p] = jnp.exp(-time_step * (own + coupling * value - energy_shift))
            return 0

        lax.fori_loop(0, PL, mix, 0)

    start_all(functools.partial(g_copy, 0), M)
    for which, out in ((1, residual_out), (0, density_out)):
        for r in range(M):
            mm = lax.rem(m + M - r, M)
            if r > 0:
                g_copy(which, r).wait_recv()

            def widen(p, _, which=which, mm=mm):
                staged[which, mm, p] = gath[which, mm, p].astype(F32)
                return 0

            lax.fori_loop(0, PL, widen, 0)
            pltpu.make_async_copy(
                staged.at[which, mm], out.at[pl.ds(mm * PL, PL)], out_sem.at[which, r]
            ).start()
    for which, out in ((1, residual_out), (0, density_out)):
        for r in range(M):
            mm = lax.rem(m + M - r, M)
            pltpu.make_async_copy(
                staged.at[which, mm], out.at[pl.ds(mm * PL, PL)], out_sem.at[which, r]
            ).wait()

    for t in range(NB):
        wait_sent(functools.partial(f_copy, t), peers)
    for k in range(K):
        wait_sent(functools.partial(b_copy, k), peers)
        for it in range(ITERS):
            wait_sent(functools.partial(e_copy, it, k), H)
    wait_sent(functools.partial(a_copy, ITERS - 1), peers)
    wait_sent(o_copy, M)
    for which in range(2):
        wait_sent(functools.partial(g_copy, which), M)


def solution(mesh):
    G = mesh.shape["grid"]
    B = mesh.shape["band"]

    def local(
        bands,
        occupations,
        external,
        density_in,
        prev_density,
        prev_residual,
        hist_density,
        hist_residual,
    ):
        NB = bands.shape[1]
        S, NG = external.shape[0], external.shape[1]
        M = max(1, min(B, S // 8))
        H = B // M
        PL = S // M
        C = NG // 2 // G
        K = min(4, PL)
        PB = PL // K
        dims = (G, M, H, NB, PL, C, K, PB, NG)
        peers = G * M
        hbm = pl.BlockSpec(memory_space=pl.ANY)
        vmem = pl.BlockSpec(memory_space=pltpu.VMEM)
        smem = pl.BlockSpec(memory_space=pltpu.SMEM)
        field = jax.ShapeDtypeStruct((S, NG, NG), F32)
        dma = pltpu.SemaphoreType.DMA
        loads = 2 + NB * M * 2 + 3 + 2 * (DEPTH - 1)
        scratch = [
            pltpu.VMEM((NB, M, 2, PL, NG, NG), BF),
            pltpu.VMEM((NB, G, M, PL, C, NG), BF),
            pltpu.VMEM((NB, G, M, PL, C, NG), BF),
            pltpu.VMEM((K, G, M, PB, NB, C, NG), BF),
            pltpu.VMEM((K, M, G, PB, NB, C, NG), BF),
            pltpu.VMEM((NG * (C + 8), NG), F32),
            pltpu.VMEM((C * (NG + 8), NG), F32),
            pltpu.VMEM((M, PL, NG, NG), F32),
            pltpu.VMEM((S, NG, NG), F32),
            pltpu.VMEM((S, NG, NG), F32),
            pltpu.VMEM((DEPTH, PL, NG, NG), F32),
            pltpu.VMEM((DEPTH, PL, NG, NG), F32),
            pltpu.VMEM((ITERS, PL, NG, NG), F32),
            pltpu.VMEM((ITERS + 1, PL, NG, NG), F32),
            pltpu.VMEM((PL, NG, NG), F32),
            pltpu.VMEM((ITERS, H, PL, NG, NG), BF),
            pltpu.VMEM((ITERS, peers, 1, NG), F32),
            pltpu.VMEM((1 + DEPTH * (DEPTH + 1) // 2, 1, NG), F32),
            pltpu.VMEM((M, NB, 1, NG), F32),
            pltpu.VMEM((2, M, PL, NG, NG), BF),
            pltpu.VMEM((2, M, PL, NG, NG), F32),
            dma((loads,)),
            dma((NB, G)),
            dma((NB, G)),
            dma((NB, peers)),
            dma((NB, peers)),
            dma((K, peers)),
            dma((K, peers)),
            dma((ITERS, K, H)),
            dma((ITERS, K, H)),
            dma((peers,)),
            dma((peers,)),
            dma((M,)),
            dma((M,)),
            dma((2, M)),
            dma((2, M)),
            dma((2, M)),
        ]
        return pl.pallas_call(
            functools.partial(kernel, dims),
            in_specs=[smem] + [hbm] * 7 + [vmem] * 6,
            out_specs=(hbm, hbm),
            out_shape=(field, field),
            scratch_shapes=scratch,
            compiler_params=pltpu.CompilerParams(
                collective_id=0, has_side_effects=True, vmem_limit_bytes=60 * 1024 * 1024
            ),
            name="scf",
        )(
            occupations,
            bands,
            external,
            density_in,
            prev_density,
            prev_residual,
            hist_density,
            hist_residual,
            *make_tables(NG),
        )

    placed = (
        P(None, "band", "grid", None, None),
        P("band"),
        P("grid", None, None),
        P("grid", None, None),
        P("grid", None, None),
        P("grid", None, None),
        P(None, "grid", None, None),
        P(None, "grid", None, None),
    )
    return jax.shard_map(
        local,
        mesh=mesh,
        in_specs=placed,
        out_specs=(P("grid", None, None), P("grid", None, None)),
        check_vma=False,
    )
```

time: 598 us -> 184 us (0.31); the launches traced: 588 us -> 183 us
  waiting for transfers between devices: 234 us -> 0 us
  Pallas kernels: 54 us -> 178 us
  blocking collectives: 110 us -> 0 us
  local copies, waits for them, and re-layouts: 90.4 us -> 4.61 us
  other arithmetic: 52.7 us -> 0 us
  matrix products: 28 us -> 0 us
  between operations: 14.4 us -> 0.65 us
    psum x3 -> x0, waiting for transfers between devices: 221 us -> none  [local(): lax.psum((jnp.sum(weighted_sq, axis=0) * (density_scale / bands_total)).a...]
    pallas_call x7 -> x1, Pallas kernels: 54 us -> 178 us  [local(): pl.pallas_call(functools.partial(kernel, dims), in_specs=[smem] + [hbm] *...]
    all_to_all x5 -> x0, blocking collectives: 89 us -> none  [the longest x3 53.2 us: local(): lax.all_to_all(spatial.astype(jnp.bfloat16).reshape(item_count, column_ro...]
    reshape x20 -> x0, local copies, waits for them, and re-layouts: 67.6 us -> none  [the longest x6 28 us: local(): returned.reshape(band_items, kept_count, slab_planes, 2, kept_count)]
    dot_general x15 -> x0, matrix products: 28 us -> none  [the longest x3 8.5 us: local(): jnp.einsum('bykdz,dkcx->byxcz', damped, inverse_axis, preferred_element_t...]
    exp x3 -> x0, other arithmetic: 28 us -> none  [local(): jnp.exp(-time_step * (external + coupling * density_now - energy_shift))]
    psum x3 -> x0, blocking collectives: 21.5 us -> none  [the longest x2 14 us: local(): sums = lax.psum(jnp.sum(partial, axis=(1, 2)) / cells_total, 'grid')]
    all_to_all x1 -> x0, waiting for transfers between devices: 13.5 us -> none  [local(): lax.all_to_all(along_y, 'grid', split_axis=1, concat_axis=2, tiled=True)]
  transfers between devices with their start and end apart: 4 -> 0, of which waited for: 4 -> 0; matrix products, arithmetic and copies ran while one was open for 0% -> 0% of each run, Pallas kernels for 2% -> 0%
where the time goes in v1:
time: 184 us; the launch traced here: 183 us
  Pallas kernels  178 us (97%)
  local copies, waits for them, and re-layouts  4.61 us (3%)
    pallas_call x1, Pallas kernels, local(): pl.pallas_call(functools.partial(kernel, dims), in_specs=[smem] + [hbm] *...  178 us
    unnamed x4, local copies, waits for them, and re-layouts  4.61 us

profile of v1, /device:TPU:0, one launch (start us, length us, event | category | flops | bytes accessed | tf_op | source)
XLA Modules:
  0.0 183.4 jit_solution(3263212896373191590)
XLA Ops:
  0.6 178.1 %scf.1 = (f32[32,128,128]{2,1,0:T(8,128)}, f32[32,128,128]{2,1,0:T(8,128)}) custom-call(f32[2]{0:T(128)} %occ_in.1, bf16[2,2,32,128,128]{4,3,2,1,0:T(8,128)(2,1)} %bands.1, f32[32,128,128]{2,1,0:T(8,128)} %external.1, f32[32,128,128]{2,1,0:T(8,128)} %density_in.1, f32[32,128,128]{2,1,0:T(8,128)} %prev_density.1, f32[32,128,128]{2,1,0:T(8,128)} %prev_residual.1, ...), custom_call_target="tpu_custom_call" | custom-call | tf_op jit(solution)/shard_map/scf/pallas_call | solution.py:649
  178.8 0.0 copy-start
  178.8 3.3 %copy.18 = f32[32,128,128]{2,1,0:T(8,128)} copy(f32[32,128,128]{2,1,0:T(8,128)} %get-tuple-element.4) | data formatting | bytes 4194304
  182.1 0.0 copy-done
  182.1 1.3 copy.19
Async XLA Ops:
  178.8 3.3 %copy-start = (f32[32,128,128]{2,1,0:T(8,128)S(1)}, f32[32,128,128]{2,1,0:T(8,128)}, u32[]{:S(2)}) copy-start(f32[32,128,128]{2,1,0:T(8,128)} %get-tuple-element.5) | copy-start | bytes 6291460

commit v2 on v1

--- a/solution.py
+++ b/solution.py
@@ -1,3 +1,4 @@
+import contextlib
 import functools
 import math
 
@@ -21,6 +22,11 @@
 density_scale = 8.0
 
 MESH = pl.DeviceIdType.MESH
+
+
+def mark(name):
+    return contextlib.nullcontext()
+
 BF = jnp.bfloat16
 F32 = jnp.float32
 
@@ -35,6 +41,7 @@
         [np.concatenate([cos, -sin, -sin, -cos], 1), np.concatenate([sin, cos, cos, -sin], 1)], 0
     )
     forward = np.concatenate([cos.T, sin.T], 1)
+    forward_x = np.concatenate([cos.T, sin.T], 0)
     inverse = np.concatenate([cos, -sin], 1)
     inverse_z = np.concatenate(
         [np.concatenate([cos.T, sin.T], 1), np.concatenate([-sin.T, cos.T], 1)], 0
@@ -48,6 +55,7 @@
     return (
         as_bf(forward_z),
         as_bf(forward),
+        as_bf(forward_x),
         as_bf(inverse),
         as_bf(inverse_z),
         jnp.asarray(pair, F32),
@@ -102,6 +110,7 @@
     hist_residual,
     fz,
     fy,
+    fx,
     iy,
     iz,
     pair_damp,
@@ -113,8 +122,13 @@
     recv_f,
     send_b,
     recv_b,
+    along_z,
     xscr,
+    xrhs,
+    crhs,
     dscr,
+    drhs,
+    erows,
     fac,
     ext,
     rho0,
@@ -128,10 +142,7 @@
     gsc,
     occ,
     gath,
-    staged,
     load_sem,
-    f1_send,
-    f1_recv,
     f_send,
     f_recv,
     b_send,
@@ -176,11 +187,17 @@
         loads.append(copy)
         return copy
 
-    first = [load(external, ext), load(density_in, rho0)]
+    first = []
     for t in range(NB):
+        group = []
         for j in range(M):
+            block = pl.ds(j * PL, PL)
+            if t == 0:
+                group.append(load(external.at[block], ext.at[block]))
+                group.append(load(density_in.at[block], rho0.at[block]))
             for c in range(2):
-                first.append(load(bands.at[c, t, pl.ds(j * PL, PL)], psi.at[t, j, c]))
+                group.append(load(bands.at[c, t, block], psi.at[t, j, :, :, pl.ds(c * NG, NG)]))
+        first.append(group)
     mine = pl.ds(m * PL, PL)
     later = [
         load(density_in.at[mine], now.at[0]),
@@ -213,27 +230,39 @@
     def rot(x):
         return pltpu.roll(x, NG // 2, 1) * sign
 
-    def f1_copy(t, r):
-        gg = lax.rem(g + r, G)
+    def f_copy(t, gg, j, slot, mm):
         return pltpu.make_async_remote_copy(
-            src_ref=send_f.at[t, gg],
-            dst_ref=recv_f.at[t, g],
-            send_sem=f1_send.at[t, r],
-            recv_sem=f1_recv.at[t, r],
-            device_id=(b, gg),
-            device_id_type=MESH,
-        )
-
-    def f_copy(t, r):
-        mm, gg = place(r)
-        return pltpu.make_async_remote_copy(
-            src_ref=send_f.at[t, gg, mm],
-            dst_ref=recv_f.at[t, g, m],
-            send_sem=f_send.at[t, r],
-            recv_sem=f_recv.at[t, r],
+            src_ref=send_f.at[t, gg * M + j],
+            dst_ref=recv_f.at[t, slot],
+            send_sem=f_send.at[t, gg * M + j],
+            recv_sem=f_recv.at[t, slot],
             device_id=device(mm, gg),
             device_id_type=MESH,
         )
+
+    own = g * M + m
+
+    def f_arrived(it, t):
+        lowest = M if it == 0 else 1
+        base = g * M if it == 0 else own
+
+        def body(r, _):
+            slot = lax.rem(base + r, peers)
+            f_copy(t, slot // M, lax.rem(slot, M), slot, m).wait_recv()
+            return 0
+
+        lax.fori_loop(lowest, peers, body, 0)
+
+    def f_sent(it, t):
+        lowest = M if it == 0 else 1
+        base = g * M if it == 0 else own
+
+        def body(r, _):
+            slot = lax.rem(base + r, peers)
+            f_copy(t, slot // M, lax.rem(slot, M), slot, m).wait_send()
+            return 0
+
+        lax.fori_loop(lowest, peers, body, 0)
 
     def b_copy(k, r):
         mm, gg = place(r)
@@ -280,13 +309,14 @@
             device_id_type=MESH,
         )
 
-    def g_copy(which, r):
+    def g_copy(which, k, r):
         mm = lax.rem(m + r, M)
+        rows = pl.ds(k * PB, PB)
         return pltpu.make_async_remote_copy(
-            src_ref=gath.at[which, m],
-            dst_ref=gath.at[which, m],
-            send_sem=g_send.at[which, r],
-            recv_sem=g_recv.at[which, r],
+            src_ref=gath.at[which, m, rows],
+            dst_ref=gath.at[which, m, rows],
+            send_sem=g_send.at[which, k, r],
+            recv_sem=g_recv.at[which, k, r],
             device_id=device(mm, g),
             device_id_type=MESH,
         )
@@ -312,97 +342,108 @@
 
         lax.fori_loop(1, count, body, 0)
 
-    def forward_zy(t, per_block):
-        def body(j, _):
-            place_of = j if per_block else 0
+    def forward_zy(it, t):
+        def make(j):
+            at = j if it == 0 else 0
+            for q in range(PL):
+                f = fac[at, q]
+                real = (psi[t, j, q, :, :NG].astype(F32) * f).astype(BF)
+                imag = (psi[t, j, q, :, NG:].astype(F32) * f).astype(BF)
+                along_z[q] = dot(jnp.concatenate([real, imag], axis=1), fz[...]).astype(BF)
             for two in range(PL // 2):
-                rows = []
-                for q in (2 * two, 2 * two + 1):
-                    f = fac[place_of, q]
-                    real = (psi[t, j, 0, q].astype(F32) * f).astype(BF)
-                    imag = (psi[t, j, 1, q].astype(F32) * f).astype(BF)
-                    rows.append(jnp.concatenate([real, imag], axis=1))
-                along = dot(jnp.concatenate(rows, axis=0), fz[...]).astype(BF)
-                top = jnp.concatenate([along[:NG, :NG], along[NG:, :NG]], axis=1)
-                low = jnp.concatenate([along[:NG, NG:], along[NG:, NG:]], axis=1)
+                even, odd = along_z[2 * two], along_z[2 * two + 1]
+                top = jnp.concatenate([even[:, :NG], odd[:, :NG]], axis=1)
+                low = jnp.concatenate([even[:, NG:], odd[:, NG:]], axis=1)
                 out = dot(fy[...], jnp.concatenate([top, low], axis=0)).astype(BF)
                 for side in range(2):
                     for gg in range(G):
-                        send_f[t, gg, j, 2 * two + side] = out[
+                        send_f[t, gg * M + j, 2 * two + side] = out[
                             gg * C : (gg + 1) * C, side * NG : (side + 1) * NG
                         ]
-            return 0
-
-        lax.fori_loop(0, M, body, 0)
+
+        def send(j, lowest):
+            def body(r, _):
+                gg = lax.rem(g + r, G)
+                if it == 0:
+                    f_copy(t, gg, j, g * M + j, m).start()
+                else:
+                    f_copy(t, gg, j, own, j).start()
+                return 0
+
+            lax.fori_loop(lowest, G, body, 0)
+
+        def step(n, _):
+            j = lax.rem(m + 1 + n, M)
+            make(j)
+            send(j, 1 if it == 0 else 0)
+            if it == 0:
+                recv_f[t, g * M + j] = send_f[t, g * M + j]
+            return 0
+
+        if it == 0:
+            lax.fori_loop(0, M, step, 0)
+        else:
+            lax.fori_loop(0, M - 1, step, 0)
+            make(m)
+            send(m, 1)
+            recv_f[t, own] = send_f[t, own]
 
     def spectral(t):
         def spread(blk, _):
-            gg, mm = blk // M, lax.rem(blk, M)
             for p in range(PL):
                 start = pl.multiple_of((blk * PL + p) * xs, 8)
-                xscr[pl.ds(start, C), :] = recv_f[t, gg, mm, p].astype(F32)
+                xscr[pl.ds(start, C), :] = recv_f[t, blk, p].astype(F32)
             return 0
 
         lax.fori_loop(0, peers, spread, 0)
-        unroll = min(4, C)
-
-        def columns(part, _):
-            for two in range(unroll // 2):
-                stacked = []
-                for side in range(2):
-                    kl = part * unroll + two * 2 + side
-                    x = xscr[pl.ds(kl, NG, stride=xs), :]
-                    stacked.append(jnp.concatenate([x.astype(BF), rot(x).astype(BF)], axis=0))
-                c = dot(fy[...], jnp.concatenate(stacked, axis=1))
-                stacked = []
-                for side in range(2):
-                    kl = part * unroll + two * 2 + side
-                    damp = pair_damp[...] * single_damp[pl.ds(g * C + kl, 1), :]
-                    one = c[:, side * NG : (side + 1) * NG] * damp
-                    stacked.append(jnp.concatenate([one.astype(BF), rot(one).astype(BF)], axis=0))
-                d = dot(iy[...], jnp.concatenate(stacked, axis=1))
-                for side in range(2):
-                    kl = part * unroll + two * 2 + side
-                    start = pl.multiple_of(kl * ds, 8)
-                    dscr[pl.ds(start, NG), :] = d[:, side * NG : (side + 1) * NG]
-            return 0
-
-        lax.fori_loop(0, C // unroll, columns, 0)
-
-        def collect(blk, _):
-            gg, mm = blk // M, lax.rem(blk, M)
-            for p in range(PL):
-                v = dscr[pl.ds(blk * PL + p, C, stride=ds), :]
-                send_b[p // PB, gg, mm, p % PB, t] = v.astype(BF)
-            return 0
-
-        lax.fori_loop(0, peers, collect, 0)
+        for kl in range(C):
+            xrhs[:, kl * NG : (kl + 1) * NG] = xscr[pl.ds(kl, NG, stride=xs), :].astype(BF)
+        for two in range(C // 2):
+            c = dot(fx[...], xrhs[:, two * 2 * NG : (two + 1) * 2 * NG])
+            for side in range(2):
+                kl = 2 * two + side
+                lanes = slice(side * NG, (side + 1) * NG)
+                damp = pair_damp[...] * single_damp[pl.ds(g * C + kl, 1), :]
+                one = (c[:kept, lanes] + rot(c[kept:, lanes])) * damp
+                crhs[:kept, kl * NG : (kl + 1) * NG] = one.astype(BF)
+                crhs[kept:, kl * NG : (kl + 1) * NG] = rot(one).astype(BF)
+        for two in range(C // 2):
+            d = dot(iy[...], crhs[:, two * 2 * NG : (two + 1) * 2 * NG])
+            for side in range(2):
+                kl = 2 * two + side
+                dscr[kl * ds : kl * ds + NG, :] = d[:, side * NG : (side + 1) * NG]
+
+    def collect(t, k):
+        def body(blk, _):
+            for pp in range(PB):
+                v = dscr[pl.ds(blk * PL + k * PB + pp, C, stride=ds), :]
+                send_b[k, blk // M, lax.rem(blk, M), pp, t] = v.astype(BF)
+            return 0
+
+        lax.fori_loop(0, peers, body, 0)
 
     def inverse_yz(it, k):
-        keep = it < ITERS - 1
-
         def body(pp, _):
             p = k * PB + pp
+            count = NB * M
+            for n in range(count):
+                d = jnp.concatenate(
+                    [recv_b[k, n // NB, gg, pp, n % NB].astype(F32) for gg in range(G)], axis=0
+                )
+                drhs[:kept, n * NG : (n + 1) * NG] = d.astype(BF)
+                drhs[kept:, n * NG : (n + 1) * NG] = rot(d).astype(BF)
+            for two in range(count // 2):
+                e = dot(iy[...], drhs[:, two * 2 * NG : (two + 1) * 2 * NG]).astype(BF)
+                for side in range(2):
+                    n = 2 * two + side
+                    erows[n * NG : (n + 1) * NG, :] = e[:, side * NG : (side + 1) * NG]
+            for n in range(count):
+                psi[n % NB, n // NB, p] = dot(erows[n * NG : (n + 1) * NG, :], iz[...]).astype(BF)
             total = jnp.zeros((NG, NG), F32)
-            for j in range(M):
-                stacked = []
-                for t in range(NB):
-                    d = jnp.concatenate(
-                        [recv_b[k, j, gg, pp, t].astype(F32) for gg in range(G)], axis=0
-                    )
-                    stacked.append(jnp.concatenate([d.astype(BF), rot(d).astype(BF)], axis=0))
-                e = dot(iy[...], jnp.concatenate(stacked, axis=1)).astype(BF)
-                e = jnp.concatenate([e[:, t * NG : (t + 1) * NG] for t in range(NB)], axis=0)
-                wave = dot(e, iz[...]).astype(BF)
-                for t in range(NB):
-                    real = wave[t * NG : (t + 1) * NG, :NG]
-                    imag = wave[t * NG : (t + 1) * NG, NG:]
-                    if keep:
-                        psi[t, j, 0, p] = real
-                        psi[t, j, 1, p] = imag
-                    real = real.astype(F32)
-                    imag = imag.astype(F32)
-                    total = total + occ[j, t] * (real * real + imag * imag)
+            for n in range(count):
+                real = psi[n % NB, n // NB, p, :, :NG].astype(F32)
+                imag = psi[n % NB, n // NB, p, :, NG:].astype(F32)
+                total = total + occ[n // NB, n % NB] * (real * real + imag * imag)
             parts[it, h, p] = (total * (density_scale / (NB * M * H))).astype(BF)
             return 0
 
@@ -411,8 +452,9 @@
     for t in range(NB):
         occ[m, t] = jnp.full((1, NG), occ_in[t], F32)
 
-    for copy in first:
-        copy.wait()
+    with mark("loads"):
+        for copy in first[0]:
+            copy.wait()
 
     def first_factor(j, _):
         for q in range(PL):
@@ -420,28 +462,25 @@
             fac[j, q] = jnp.exp(-time_step * (ext[plane] + coupling * rho0[plane] - energy_shift))
         return 0
 
-    lax.fori_loop(0, M, first_factor, 0)
+    with mark("factor"):
+        lax.fori_loop(0, M, first_factor, 0)
+    with mark("barrier"):
+        pl.semaphore_wait(barrier, peers - 1 + H - 1)
+    start_all(o_copy, M)
 
     cells = 1.0 / (NG * NG * NG)
     for it in range(ITERS):
         slot = (DEPTH - 1 + it) % DEPTH
-        forward_make = f1_copy if it == 0 else f_copy
-        forward_count = G if it == 0 else peers
         for t in range(NB):
-            if it > 0:
-                wait_sent(functools.partial(f1_copy if it == 1 else f_copy, t), G if it == 1 else peers)
-            forward_zy(t, it == 0)
-            if it == 0 and t == 0:
-                pl.semaphore_wait(barrier, peers - 1 + H - 1)
-                start_all(o_copy, M)
-            start_all(functools.partial(forward_make, t), forward_count)
-            if it == 0:
-                recv_f[t, g] = send_f[t, g]
-            else:
-                recv_f[t, g, m] = send_f[t, g, m]
+            if it == 0 and t > 0:
+                for copy in first[t]:
+                    copy.wait()
+            with mark(f"F{t}"):
+                forward_zy(it, t)
         if it == 0:
-            for copy in later:
-                copy.wait()
+            with mark("later"):
+                for copy in later:
+                    copy.wait()
 
             def prepare(p, accs):
                 entries = [q_hist[j, p] for j in range(DEPTH - 1)]
@@ -453,31 +492,39 @@
                 return tuple(out)
 
             zeros = tuple(jnp.zeros((8, NG), F32) for _ in range(spot(DEPTH - 1, 0)))
-            kept_sums = lax.fori_loop(0, PL, prepare, zeros)
+            with mark("prepare"):
+                kept_sums = lax.fori_loop(0, PL, prepare, zeros)
             line = jnp.zeros((1, NG), F32)
             for n, acc in enumerate(kept_sums):
                 value = jnp.sum(jnp.sum(acc, axis=0, keepdims=True), axis=1, keepdims=True)
                 line = line + jnp.where(lane == 2 * DEPTH + n, value, 0.0)
             gsc[0] = line
         for t in range(NB):
-            wait_arrived(functools.partial(forward_make, t), forward_count)
-            if it > 0 and t == 0:
-                for k in range(K):
-                    wait_sent(functools.partial(b_copy, k), peers)
-            spectral(t)
-        for k in range(K):
-            start_all(functools.partial(b_copy, k), peers)
-            recv_b[k, m, g] = send_b[k, g, m]
+            with mark(f"waitF{t}"):
+                f_arrived(it, t)
+            with mark(f"X{t}"):
+                spectral(t)
+            for k in range(K):
+                with mark(f"collect{t}{k}"):
+                    collect(t, k)
+                    if t == NB - 1:
+                        start_all(functools.partial(b_copy, k), peers)
+                        recv_b[k, m, g] = send_b[k, g, m]
+        for t in range(NB):
+            f_sent(it, t)
         if it == 0:
             wait_arrived(o_copy, M)
         for k in range(K):
-            wait_arrived(functools.partial(b_copy, k), peers)
-            inverse_yz(it, k)
+            with mark(f"waitB{k}"):
+                wait_arrived(functools.partial(b_copy, k), peers)
+            with mark(f"C{k}"):
+                inverse_yz(it, k)
             start_all(functools.partial(e_copy, it, k), H)
 
         accs = tuple(jnp.zeros((8, NG), F32) for _ in range(2 * DEPTH))
         for k in range(K):
-            wait_arrived(functools.partial(e_copy, it, k), H)
+            with mark(f"waitE{k}"):
+                wait_arrived(functools.partial(e_copy, it, k), H)
 
             def gather_sums(p, accs, it=it, slot=slot):
                 rho = parts[it, 0, p].astype(F32)
@@ -499,18 +546,23 @@
                     gath[1, m, p] = residual.astype(BF)
                 return tuple(out)
 
-            accs = lax.fori_loop(k * PB, (k + 1) * PB, gather_sums, accs)
-        if it == ITERS - 1:
-            start_all(functools.partial(g_copy, 1), M)
+            with mark(f"gram{k}"):
+                accs = lax.fori_loop(k * PB, (k + 1) * PB, gather_sums, accs)
+            if it == ITERS - 1 and k < K - 1:
+                start_all(functools.partial(g_copy, 1, k), M)
         line = gsc[0] if it == 0 else jnp.zeros((1, NG), F32)
         for n, acc in enumerate(accs):
             value = jnp.sum(jnp.sum(acc, axis=0, keepdims=True), axis=1, keepdims=True)
             line = line + jnp.where(lane == n, value, 0.0)
-        if it > 0:
-            wait_sent(functools.partial(a_copy, it - 1), peers)
         sums[it, rank] = line
         start_all(functools.partial(a_copy, it), peers)
-        wait_arrived(functools.partial(a_copy, it), peers)
+        if it == ITERS - 1:
+            start_all(functools.partial(g_copy, 1, K - 1), M)
+        for k in range(K):
+            wait_sent(functools.partial(b_copy, k), peers)
+            wait_sent(functools.partial(e_copy, it, k), H)
+        with mark("waitA"):
+            wait_arrived(functools.partial(a_copy, it), peers)
         total = sums[it, 0]
         for r in range(1, peers):
             total = total + sums[it, r]
@@ -527,7 +579,8 @@
         for j in range(DEPTH):
             gsc[1 + spot(j, slot)] = pick(j)
         gram = {(j, kk): gsc[1 + spot(j, kk)] for j in range(DEPTH) for kk in range(j + 1)}
-        coeffs = solve(gram, vector)
+        with mark("solve"):
+            coeffs = solve(gram, vector)
 
         def mix(p, _, it=it, coeffs=coeffs):
             value = now[it, p] + mixing_weight * res[it + 1, p]
@@ -541,40 +594,34 @@
                 fac[0, p] = jnp.exp(-time_step * (own + coupling * value - energy_shift))
             return 0
 
-        lax.fori_loop(0, PL, mix, 0)
-
-    start_all(functools.partial(g_copy, 0), M)
-    for which, out in ((1, residual_out), (0, density_out)):
+        wait_sent(functools.partial(a_copy, it), peers)
+        with mark("mix"):
+            for k in range(K):
+                lax.fori_loop(k * PB, (k + 1) * PB, mix, 0)
+                if it == ITERS - 1:
+                    start_all(functools.partial(g_copy, 0, k), M)
+
+    def out_copy(which, r):
+        mm = lax.rem(m + M - r, M)
+        out = density_out if which == 0 else residual_out
+        return pltpu.make_async_copy(
+            gath.at[which, mm], out.at[pl.ds(mm * PL, PL)], out_sem.at[which, r]
+        )
+
+    for which in (1, 0):
         for r in range(M):
-            mm = lax.rem(m + M - r, M)
             if r > 0:
-                g_copy(which, r).wait_recv()
-
-            def widen(p, _, which=which, mm=mm):
-                staged[which, mm, p] = gath[which, mm, p].astype(F32)
-                return 0
-
-            lax.fori_loop(0, PL, widen, 0)
-            pltpu.make_async_copy(
-                staged.at[which, mm], out.at[pl.ds(mm * PL, PL)], out_sem.at[which, r]
-            ).start()
-    for which, out in ((1, residual_out), (0, density_out)):
+                with mark(f"waitG{which}{r}"):
+                    for k in range(K):
+                        g_copy(which, k, r).wait_recv()
+            out_copy(which, r).start()
+    for which in (1, 0):
         for r in range(M):
-            mm = lax.rem(m + M - r, M)
-            pltpu.make_async_copy(
-                staged.at[which, mm], out.at[pl.ds(mm * PL, PL)], out_sem.at[which, r]
-            ).wait()
-
-    for t in range(NB):
-        wait_sent(functools.partial(f_copy, t), peers)
-    for k in range(K):
-        wait_sent(functools.partial(b_copy, k), peers)
-        for it in range(ITERS):
-            wait_sent(functools.partial(e_copy, it, k), H)
-    wait_sent(functools.partial(a_copy, ITERS - 1), peers)
+            out_copy(which, r).wait()
     wait_sent(o_copy, M)
     for which in range(2):
-        wait_sent(functools.partial(g_copy, which), M)
+        for k in range(K):
+            wait_sent(functools.partial(g_copy, which, k), M)
 
 
 def solution(mesh):
@@ -604,17 +651,23 @@
         hbm = pl.BlockSpec(memory_space=pl.ANY)
         vmem = pl.BlockSpec(memory_space=pltpu.VMEM)
         smem = pl.BlockSpec(memory_space=pltpu.SMEM)
-        field = jax.ShapeDtypeStruct((S, NG, NG), F32)
+        field = jax.ShapeDtypeStruct((S, NG, NG), BF)
         dma = pltpu.SemaphoreType.DMA
-        loads = 2 + NB * M * 2 + 3 + 2 * (DEPTH - 1)
+        loads = 2 * M + NB * M * 2 + 3 + 2 * (DEPTH - 1)
+        bands_held = NB * M
         scratch = [
-            pltpu.VMEM((NB, M, 2, PL, NG, NG), BF),
-            pltpu.VMEM((NB, G, M, PL, C, NG), BF),
-            pltpu.VMEM((NB, G, M, PL, C, NG), BF),
+            pltpu.VMEM((NB, M, PL, NG, 2 * NG), BF),
+            pltpu.VMEM((NB, peers, PL, C, NG), BF),
+            pltpu.VMEM((NB, peers, PL, C, NG), BF),
             pltpu.VMEM((K, G, M, PB, NB, C, NG), BF),
             pltpu.VMEM((K, M, G, PB, NB, C, NG), BF),
+            pltpu.VMEM((PL, NG, 2 * NG), BF),
             pltpu.VMEM((NG * (C + 8), NG), F32),
+            pltpu.VMEM((NG, C * NG), BF),
+            pltpu.VMEM((NG, C * NG), BF),
             pltpu.VMEM((C * (NG + 8), NG), F32),
+            pltpu.VMEM((NG, bands_held * NG), BF),
+            pltpu.VMEM((bands_held * NG, NG), BF),
             pltpu.VMEM((M, PL, NG, NG), F32),
             pltpu.VMEM((S, NG, NG), F32),
             pltpu.VMEM((S, NG, NG), F32),
@@ -628,10 +681,7 @@
             pltpu.VMEM((1 + DEPTH * (DEPTH + 1) // 2, 1, NG), F32),
             pltpu.VMEM((M, NB, 1, NG), F32),
             pltpu.VMEM((2, M, PL, NG, NG), BF),
-            pltpu.VMEM((2, M, PL, NG, NG), F32),
             dma((loads,)),
-            dma((NB, G)),
-            dma((NB, G)),
             dma((NB, peers)),
             dma((NB, peers)),
             dma((K, peers)),
@@ -642,13 +692,13 @@
             dma((peers,)),
             dma((M,)),
             dma((M,)),
-            dma((2, M)),
-            dma((2, M)),
+            dma((2, K, M)),
+            dma((2, K, M)),
             dma((2, M)),
         ]
-        return pl.pallas_call(
+        density, residual = pl.pallas_call(
             functools.partial(kernel, dims),
-            in_specs=[smem] + [hbm] * 7 + [vmem] * 6,
+            in_specs=[smem] + [hbm] * 7 + [vmem] * 7,
             out_specs=(hbm, hbm),
             out_shape=(field, field),
             scratch_shapes=scratch,
@@ -667,6 +717,7 @@
             hist_residual,
             *make_tables(NG),
         )
+        return density.astype(F32), residual.astype(F32)
 
     placed = (
         P(None, "band", "grid", None, None),

time: 184 us -> 161 us (0.88)
  Pallas kernels: 178 us -> 156 us
  local copies, waits for them, and re-layouts: 4.61 us -> 0.01 us
  other arithmetic: 0 us -> 4.43 us
    pallas_call x1, Pallas kernels: 178 us -> 156 us  [local(): pl.pallas_call(functools.partial(kernel, dims), in_specs=[smem] + [hbm] *...]
    unnamed x4 -> x2, local copies, waits for them, and re-layouts: 4.61 us -> 0.01 us
    convert_element_type x0 -> x2, other arithmetic: none -> 4.43 us  [local(): return (density.astype(F32), residual.astype(F32))]
where the time goes in v2:
time: 161 us
  Pallas kernels  156 us (97%)
  other arithmetic  4.43 us (3%)
    pallas_call x1, Pallas kernels, local(): pl.pallas_call(functools.partial(kernel, dims), in_specs=[smem] + [hbm] *...  156 us
    convert_element_type x2, other arithmetic, local(): return (density.astype(F32), residual.astype(F32))  4.43 us

profile of v2, /device:TPU:0, one launch (start us, length us, event | category | flops | bytes accessed | tf_op | source)
XLA Modules:
  0.0 161.2 jit_solution(10161688323796360473)
XLA Ops:
  0.6 156.1 %scf.1 = (bf16[32,128,128]{2,1,0:T(8,128)(2,1)}, bf16[32,128,128]{2,1,0:T(8,128)(2,1)}) custom-call(f32[2]{0:T(128)} %occ_in.1, bf16[2,2,32,128,128]{4,3,2,1,0:T(8,128)(2,1)} %bands.1, f32[32,128,128]{2,1,0:T(8,128)} %external.1, f32[32,128,128]{2,1,0:T(8,128)} %density_in.1, f32[32,128,128]{2,1,0:T(8,128)} %prev_density.1, f32[32,128,128]{2,1,0:T(8,128)} %prev_residual.1, ...), custom_call_target="tpu_custom_call" | custom-call | tf_op jit(solution)/shard_map/scf/pallas_call | solution.py:699
  156.8 0.0 copy-start
  156.8 2.9 %convert_element_type.26 = f32[32,128,128]{2,1,0:T(8,128)} convert(bf16[32,128,128]{2,1,0:T(8,128)(2,1)} %get-tuple-element.4) | non-fusion elementwise | flops 524288 | bytes 3145728 | tf_op jit(solution)/shard_map/convert_element_type | solution.py:720
  159.7 0.0 copy-done
  159.7 1.6 convert_element_type.27
Async XLA Ops:
  156.8 2.9 %copy-start = (bf16[32,128,128]{2,1,0:T(8,128)(2,1)S(1)}, bf16[32,128,128]{2,1,0:T(8,128)(2,1)}, u32[]{:S(2)}) copy-start(bf16[32,128,128]{2,1,0:T(8,128)(2,1)} %get-tuple-element.5) | copy-start | bytes 3145732

commit v3 on v2

--- a/solution.py
+++ b/solution.py
@@ -108,6 +108,15 @@
     prev_residual,
     hist_density,
     hist_residual,
+    fz_in,
+    fy_in,
+    fx_in,
+    iy_in,
+    iz_in,
+    pair_in,
+    single_in,
+    density_out,
+    residual_out,
     fz,
     fy,
     fx,
@@ -115,8 +124,6 @@
     iz,
     pair_damp,
     single_damp,
-    density_out,
-    residual_out,
     psi,
     send_f,
     recv_f,
@@ -142,6 +149,9 @@
     gsc,
     occ,
     gath,
+    table_sem,
+    field_sem,
+    band_sem,
     load_sem,
     f_send,
     f_recv,
@@ -155,9 +165,13 @@
     o_recv,
     g_send,
     g_recv,
+    r_send,
+    r_recv,
     out_sem,
 ):
-    G, M, H, NB, PL, C, K, PB, NG = dims
+    G, M, H, NB, PL, C, K, PB, GK, NG = dims
+    GP = PL // GK
+    relay = M == 4 and GP % 2 == 0
     kept = C * G
     peers = G * M
     xs = C + 8
@@ -187,17 +201,46 @@
         loads.append(copy)
         return copy
 
-    first = []
-    for t in range(NB):
-        group = []
-        for j in range(M):
-            block = pl.ds(j * PL, PL)
-            if t == 0:
-                group.append(load(external.at[block], ext.at[block]))
-                group.append(load(density_in.at[block], rho0.at[block]))
+    tables = [
+        pltpu.make_async_copy(src, dst, table_sem.at[n])
+        for n, (src, dst) in enumerate(
+            (
+                (fz_in, fz),
+                (fy_in, fy),
+                (fx_in, fx),
+                (iy_in, iy),
+                (iz_in, iz),
+                (pair_in, pair_damp),
+                (single_in, single_damp),
+            )
+        )
+    ]
+
+    def field_load(n, i):
+        block = pl.ds(lax.rem(m + 1 + n, M) * PL, PL)
+        src, dst = ((external, ext), (density_in, rho0))[i]
+        return pltpu.make_async_copy(src.at[block], dst.at[block], field_sem.at[i, n])
+
+    def band_load(t, n, c):
+        j = lax.rem(m + 1 + n, M)
+        return pltpu.make_async_copy(
+            bands.at[c, t, pl.ds(j * PL, PL)],
+            psi.at[t, j, :, :, pl.ds(c * NG, NG)],
+            band_sem.at[t, c, n],
+        )
+
+    for n in range(M):
+        field_load(n, 0).start()
+        field_load(n, 1).start()
+        band_load(0, n, 0).start()
+        band_load(0, n, 1).start()
+        if n == 0:
+            for copy in tables:
+                copy.start()
+    for t in range(1, NB):
+        for n in range(M):
             for c in range(2):
-                group.append(load(bands.at[c, t, block], psi.at[t, j, :, :, pl.ds(c * NG, NG)]))
-        first.append(group)
+                band_load(t, n, c).start()
     mine = pl.ds(m * PL, PL)
     later = [
         load(density_in.at[mine], now.at[0]),
@@ -229,6 +272,14 @@
 
     def rot(x):
         return pltpu.roll(x, NG // 2, 1) * sign
+
+    lanes8 = lax.broadcasted_iota(jnp.int32, (8, NG), 1)
+
+    def in_lanes(accs, offset):
+        rows = jnp.zeros((8, NG), F32)
+        for n, acc in enumerate(accs):
+            rows = rows + jnp.where(lanes8 == offset + n, jnp.sum(acc, axis=1, keepdims=True), 0.0)
+        return jnp.sum(rows, axis=0, keepdims=True)
 
     def f_copy(t, gg, j, slot, mm):
         return pltpu.make_async_remote_copy(
@@ -309,17 +360,45 @@
             device_id_type=MESH,
         )
 
+    def near(r):
+        if not relay:
+            return lax.rem(m + r, M)
+        return m + 1 - 2 * lax.rem(m, 2) if r == 1 else lax.rem(m + 2, M)
+
+    direct = (1, 2) if relay else tuple(range(1, M))
+
     def g_copy(which, k, r):
-        mm = lax.rem(m + r, M)
-        rows = pl.ds(k * PB, PB)
+        rows = pl.ds(k * GP, GP)
         return pltpu.make_async_remote_copy(
             src_ref=gath.at[which, m, rows],
             dst_ref=gath.at[which, m, rows],
             send_sem=g_send.at[which, k, r],
             recv_sem=g_recv.at[which, k, r],
-            device_id=device(mm, g),
+            device_id=device(near(r), g),
             device_id_type=MESH,
         )
+
+    def r_copy(which, k, r):
+        rows = pl.ds(k * GP + (r - 1) * (GP // 2), GP // 2)
+        block = near(r)
+        return pltpu.make_async_remote_copy(
+            src_ref=gath.at[which, block, rows],
+            dst_ref=gath.at[which, block, rows],
+            send_sem=r_send.at[which, k, r],
+            recv_sem=r_recv.at[which, k, r],
+            device_id=device(near(3 - r), g),
+            device_id_type=MESH,
+        )
+
+    def g_start(which, k):
+        for r in direct:
+            g_copy(which, k, r).start()
+
+    def g_pass_on(which, k):
+        for r in direct:
+            if relay:
+                g_copy(which, k, r).wait_recv()
+                r_copy(which, k, r).start()
 
     def start_all(make, count):
         def body(r, _):
@@ -374,6 +453,17 @@
 
         def step(n, _):
             j = lax.rem(m + 1 + n, M)
+            if it == 0:
+                band_load(t, n, 0).wait()
+                band_load(t, n, 1).wait()
+            if it == 0 and t == 0:
+                field_load(n, 0).wait()
+                field_load(n, 1).wait()
+                for q in range(PL):
+                    plane = j * PL + q
+                    fac[j, q] = jnp.exp(
+                        -time_step * (ext[plane] + coupling * rho0[plane] - energy_shift)
+                    )
             make(j)
             send(j, 1 if it == 0 else 0)
             if it == 0:
@@ -413,11 +503,11 @@
                 kl = 2 * two + side
                 dscr[kl * ds : kl * ds + NG, :] = d[:, side * NG : (side + 1) * NG]
 
-    def collect(t, k):
+    def collect(t, lowest, count):
         def body(blk, _):
-            for pp in range(PB):
-                v = dscr[pl.ds(blk * PL + k * PB + pp, C, stride=ds), :]
-                send_b[k, blk // M, lax.rem(blk, M), pp, t] = v.astype(BF)
+            for p in range(lowest, lowest + count):
+                v = dscr[pl.ds(blk * PL + p, C, stride=ds), :]
+                send_b[p // PB, blk // M, lax.rem(blk, M), p % PB, t] = v.astype(BF)
             return 0
 
         lax.fori_loop(0, peers, body, 0)
@@ -452,18 +542,8 @@
     for t in range(NB):
         occ[m, t] = jnp.full((1, NG), occ_in[t], F32)
 
-    with mark("loads"):
-        for copy in first[0]:
-            copy.wait()
-
-    def first_factor(j, _):
-        for q in range(PL):
-            plane = j * PL + q
-            fac[j, q] = jnp.exp(-time_step * (ext[plane] + coupling * rho0[plane] - energy_shift))
-        return 0
-
-    with mark("factor"):
-        lax.fori_loop(0, M, first_factor, 0)
+    for copy in tables:
+        copy.wait()
     with mark("barrier"):
         pl.semaphore_wait(barrier, peers - 1 + H - 1)
     start_all(o_copy, M)
@@ -472,9 +552,6 @@
     for it in range(ITERS):
         slot = (DEPTH - 1 + it) % DEPTH
         for t in range(NB):
-            if it == 0 and t > 0:
-                for copy in first[t]:
-                    copy.wait()
             with mark(f"F{t}"):
                 forward_zy(it, t)
         if it == 0:
@@ -494,24 +571,20 @@
             zeros = tuple(jnp.zeros((8, NG), F32) for _ in range(spot(DEPTH - 1, 0)))
             with mark("prepare"):
                 kept_sums = lax.fori_loop(0, PL, prepare, zeros)
-            line = jnp.zeros((1, NG), F32)
-            for n, acc in enumerate(kept_sums):
-                value = jnp.sum(jnp.sum(acc, axis=0, keepdims=True), axis=1, keepdims=True)
-                line = line + jnp.where(lane == 2 * DEPTH + n, value, 0.0)
-            gsc[0] = line
+            gsc[0] = in_lanes(kept_sums, 2 * DEPTH)
         for t in range(NB):
             with mark(f"waitF{t}"):
                 f_arrived(it, t)
             with mark(f"X{t}"):
                 spectral(t)
-            for k in range(K):
-                with mark(f"collect{t}{k}"):
-                    collect(t, k)
-                    if t == NB - 1:
+            with mark(f"collect{t}"):
+                if t < NB - 1:
+                    collect(t, 0, PL)
+                else:
+                    for k in range(K):
+                        collect(t, k * PB, PB)
                         start_all(functools.partial(b_copy, k), peers)
                         recv_b[k, m, g] = send_b[k, g, m]
-        for t in range(NB):
-            f_sent(it, t)
         if it == 0:
             wait_arrived(o_copy, M)
         for k in range(K):
@@ -548,16 +621,18 @@
 
             with mark(f"gram{k}"):
                 accs = lax.fori_loop(k * PB, (k + 1) * PB, gather_sums, accs)
-            if it == ITERS - 1 and k < K - 1:
-                start_all(functools.partial(g_copy, 1, k), M)
-        line = gsc[0] if it == 0 else jnp.zeros((1, NG), F32)
-        for n, acc in enumerate(accs):
-            value = jnp.sum(jnp.sum(acc, axis=0, keepdims=True), axis=1, keepdims=True)
-            line = line + jnp.where(lane == n, value, 0.0)
-        sums[it, rank] = line
+            ready = (k + 1) * PB
+            if it == ITERS - 1 and ready % GP == 0 and ready < PL:
+                g_start(1, ready // GP - 1)
+        line = in_lanes(accs, 0)
+        sums[it, rank] = gsc[0] + line if it == 0 else line
         start_all(functools.partial(a_copy, it), peers)
         if it == ITERS - 1:
-            start_all(functools.partial(g_copy, 1, K - 1), M)
+            g_start(1, GK - 1)
+            for k in range(GK - 2):
+                g_pass_on(1, k)
+        for t in range(NB):
+            f_sent(it, t)
         for k in range(K):
             wait_sent(functools.partial(b_copy, k), peers)
             wait_sent(functools.partial(e_copy, it, k), H)
@@ -596,32 +671,79 @@
 
         wait_sent(functools.partial(a_copy, it), peers)
         with mark("mix"):
-            for k in range(K):
-                lax.fori_loop(k * PB, (k + 1) * PB, mix, 0)
+            for k in range(GK):
+                lax.fori_loop(k * GP, (k + 1) * GP, mix, 0)
                 if it == ITERS - 1:
-                    start_all(functools.partial(g_copy, 0, k), M)
-
-    def out_copy(which, r):
-        mm = lax.rem(m + M - r, M)
+                    g_start(0, k)
+
+    def out_copy(which, block):
         out = density_out if which == 0 else residual_out
         return pltpu.make_async_copy(
-            gath.at[which, mm], out.at[pl.ds(mm * PL, PL)], out_sem.at[which, r]
-        )
-
+            gath.at[which, block], out.at[pl.ds(block * PL, PL)], out_sem.at[which, block]
+        )
+
+    with mark("pass"):
+        for k in range(max(GK - 2, 0), GK):
+            g_pass_on(1, k)
+        for k in range(GK):
+            g_pass_on(0, k)
     for which in (1, 0):
-        for r in range(M):
-            if r > 0:
-                with mark(f"waitG{which}{r}"):
-                    for k in range(K):
-                        g_copy(which, k, r).wait_recv()
-            out_copy(which, r).start()
+        out_copy(which, m).start()
+        for r in direct:
+            if not relay:
+                for k in range(GK):
+                    g_copy(which, k, r).wait_recv()
+            out_copy(which, near(r)).start()
+        if relay:
+            with mark(f"waitR{which}"):
+                for k in range(GK):
+                    for r in direct:
+                        r_copy(which, k, r).wait_recv()
+            out_copy(which, 3 - m).start()
     for which in (1, 0):
-        for r in range(M):
-            out_copy(which, r).wait()
+        for block in range(M):
+            out_copy(which, block).wait()
     wait_sent(o_copy, M)
     for which in range(2):
-        for k in range(K):
-            wait_sent(functools.partial(g_copy, which, k), M)
+        for k in range(GK):
+            for r in direct:
+                g_copy(which, k, r).wait_send()
+                if relay:
+                    r_copy(which, k, r).wait_send()
+
+
+def widen_kernel(blocks, density, residual, density_out, residual_out, narrow, wide, in_sem, out_sem):
+    rows = density.shape[0] // blocks
+    sources = (density, residual)
+    targets = (density_out, residual_out)
+    steps = [(w, pl.ds(n * rows, rows), n) for n in range(blocks) for w in range(2)]
+    for w, part, n in steps:
+        pltpu.make_async_copy(sources[w].at[part], narrow.at[w, part], in_sem.at[w, n]).start()
+    for w, part, n in steps:
+        pltpu.make_async_copy(sources[w].at[part], narrow.at[w, part], in_sem.at[w, n]).wait()
+        wide[w, part] = narrow[w, part].astype(F32)
+        pltpu.make_async_copy(wide.at[w, part], targets[w].at[part], out_sem.at[w, n]).start()
+    for w, part, n in steps:
+        pltpu.make_async_copy(wide.at[w, part], targets[w].at[part], out_sem.at[w, n]).wait()
+
+
+def widen(density, residual):
+    blocks = min(4, density.shape[0])
+    hbm = pl.BlockSpec(memory_space=pl.ANY)
+    field = jax.ShapeDtypeStruct(density.shape, F32)
+    return pl.pallas_call(
+        functools.partial(widen_kernel, blocks),
+        in_specs=[hbm] * 2,
+        out_specs=(hbm, hbm),
+        out_shape=(field, field),
+        scratch_shapes=[
+            pltpu.VMEM((2,) + density.shape, BF),
+            pltpu.VMEM((2,) + density.shape, F32),
+            pltpu.SemaphoreType.DMA((2, blocks)),
+            pltpu.SemaphoreType.DMA((2, blocks)),
+        ],
+        name="widen",
+    )(density, residual)
 
 
 def solution(mesh):
@@ -644,18 +766,19 @@
         H = B // M
         PL = S // M
         C = NG // 2 // G
-        K = min(4, PL)
+        K = PL
         PB = PL // K
-        dims = (G, M, H, NB, PL, C, K, PB, NG)
+        GK = min(4, PL)
+        dims = (G, M, H, NB, PL, C, K, PB, GK, NG)
         peers = G * M
         hbm = pl.BlockSpec(memory_space=pl.ANY)
-        vmem = pl.BlockSpec(memory_space=pltpu.VMEM)
         smem = pl.BlockSpec(memory_space=pltpu.SMEM)
         field = jax.ShapeDtypeStruct((S, NG, NG), BF)
         dma = pltpu.SemaphoreType.DMA
-        loads = 2 * M + NB * M * 2 + 3 + 2 * (DEPTH - 1)
+        loads = 3 + 2 * (DEPTH - 1)
+        tables = make_tables(NG)
         bands_held = NB * M
-        scratch = [
+        scratch = [pltpu.VMEM(table.shape, table.dtype) for table in tables] + [
             pltpu.VMEM((NB, M, PL, NG, 2 * NG), BF),
             pltpu.VMEM((NB, peers, PL, C, NG), BF),
             pltpu.VMEM((NB, peers, PL, C, NG), BF),
@@ -681,6 +804,9 @@
             pltpu.VMEM((1 + DEPTH * (DEPTH + 1) // 2, 1, NG), F32),
             pltpu.VMEM((M, NB, 1, NG), F32),
             pltpu.VMEM((2, M, PL, NG, NG), BF),
+            dma((len(tables),)),
+            dma((2, M)),
+            dma((NB, 2, M)),
             dma((loads,)),
             dma((NB, peers)),
             dma((NB, peers)),
@@ -692,13 +818,15 @@
             dma((peers,)),
             dma((M,)),
             dma((M,)),
-            dma((2, K, M)),
-            dma((2, K, M)),
+            dma((2, GK, M)),
+            dma((2, GK, M)),
+            dma((2, GK, M)),
+            dma((2, GK, M)),
             dma((2, M)),
         ]
         density, residual = pl.pallas_call(
             functools.partial(kernel, dims),
-            in_specs=[smem] + [hbm] * 7 + [vmem] * 7,
+            in_specs=[smem] + [hbm] * (7 + len(tables)),
             out_specs=(hbm, hbm),
             out_shape=(field, field),
             scratch_shapes=scratch,
@@ -715,9 +843,9 @@
             prev_residual,
             hist_density,
             hist_residual,
-            *make_tables(NG),
-        )
-        return density.astype(F32), residual.astype(F32)
+            *tables,
+        )
+        return widen(density, residual)
 
     placed = (
         P(None, "band", "grid", None, None),

time: 161 us -> 157 us (0.975)
  other arithmetic: 4.43 us -> 0 us
    convert_element_type x2 -> x0, other arithmetic: 4.43 us -> none  [local(): return (density.astype(F32), residual.astype(F32))]
    pallas_call x0 -> x1, Pallas kernels: none -> 3.12 us  [widen(): pl.pallas_call(functools.partial(widen_kernel, blocks), in_specs=[hbm] *...]
    pallas_call x1, Pallas kernels: 156 us -> 153 us  [local(): pl.pallas_call(functools.partial(kernel, dims), in_specs=[smem] + [hbm] *...]
where the time goes in v3:
time: 157 us
  Pallas kernels  156 us (99%)
    pallas_call x1, Pallas kernels, local(): pl.pallas_call(functools.partial(kernel, dims), in_specs=[smem] + [hbm] *...  153 us

profile of v3, /device:TPU:0, one launch (start us, length us, event | category | flops | bytes accessed | tf_op | source)
XLA Modules:
  0.0 157.1 jit_solution(12197225196809069996)
XLA Ops:
  0.6 153.2 %scf.1 = (bf16[32,128,128]{2,1,0:T(8,128)(2,1)}, bf16[32,128,128]{2,1,0:T(8,128)(2,1)}) custom-call(f32[2]{0:T(128)} %occ_in.1, bf16[2,2,32,128,128]{4,3,2,1,0:T(8,128)(2,1)} %bands.1, f32[32,128,128]{2,1,0:T(8,128)} %external.1, f32[32,128,128]{2,1,0:T(8,128)} %density_in.1, f32[32,128,128]{2,1,0:T(8,128)} %prev_density.1, f32[32,128,128]{2,1,0:T(8,128)} %prev_residual.1, ...), custom_call_target="tpu_custom_call" | custom-call | tf_op jit(solution)/shard_map/scf/pallas_call | solution.py:827
  153.8 3.1 %widen.1 = (f32[32,128,128]{2,1,0:T(8,128)}, f32[32,128,128]{2,1,0:T(8,128)}) custom-call(bf16[32,128,128]{2,1,0:T(8,128)(2,1)} %get-tuple-element.4.density, bf16[32,128,128]{2,1,0:T(8,128)(2,1)} %get-tuple-element.5.residual), custom_call_target="tpu_custom_call" | custom-call | tf_op jit(solution)/shard_map/widen/pallas_call | solution.py:734

commit v4 on v3

--- a/solution.py
+++ b/solution.py
@@ -197,7 +197,6 @@
 
     def load(src, dst):
         copy = pltpu.make_async_copy(src, dst, load_sem.at[len(loads)])
-        copy.start()
         loads.append(copy)
         return copy
 
@@ -229,18 +228,15 @@
             band_sem.at[t, c, n],
         )
 
-    for n in range(M):
+    def start_block(n):
         field_load(n, 0).start()
         field_load(n, 1).start()
         band_load(0, n, 0).start()
         band_load(0, n, 1).start()
-        if n == 0:
-            for copy in tables:
-                copy.start()
-    for t in range(1, NB):
-        for n in range(M):
-            for c in range(2):
-                band_load(t, n, c).start()
+
+    for copy in tables:
+        copy.start()
+    start_block(0)
     mine = pl.ds(m * PL, PL)
     later = [
         load(density_in.at[mine], now.at[0]),
@@ -285,43 +281,44 @@
         return pltpu.make_async_remote_copy(
             src_ref=send_f.at[t, gg * M + j],
             dst_ref=recv_f.at[t, slot],
-            send_sem=f_send.at[t, gg * M + j],
-            recv_sem=f_recv.at[t, slot],
+            send_sem=f_send.at[t],
+            recv_sem=f_recv.at[t],
             device_id=device(mm, gg),
             device_id_type=MESH,
         )
 
     own = g * M + m
 
-    def f_arrived(it, t):
-        lowest = M if it == 0 else 1
-        base = g * M if it == 0 else own
-
-        def body(r, _):
-            slot = lax.rem(base + r, peers)
-            f_copy(t, slot // M, lax.rem(slot, M), slot, m).wait_recv()
-            return 0
-
-        lax.fori_loop(lowest, peers, body, 0)
-
-    def f_sent(it, t):
-        lowest = M if it == 0 else 1
-        base = g * M if it == 0 else own
-
-        def body(r, _):
-            slot = lax.rem(base + r, peers)
-            f_copy(t, slot // M, lax.rem(slot, M), slot, m).wait_send()
-            return 0
-
-        lax.fori_loop(lowest, peers, body, 0)
+    def f_all(it, t):
+        blocks = pl.ds(0, peers - M if it == 0 else peers - 1)
+        mm, gg = place(1)
+        return pltpu.make_async_remote_copy(
+            src_ref=send_f.at[t, blocks],
+            dst_ref=recv_f.at[t, blocks],
+            send_sem=f_send.at[t],
+            recv_sem=f_recv.at[t],
+            device_id=device(mm, gg),
+            device_id_type=MESH,
+        )
 
     def b_copy(k, r):
         mm, gg = place(r)
         return pltpu.make_async_remote_copy(
-            src_ref=send_b.at[k, gg, mm],
-            dst_ref=recv_b.at[k, m, g],
-            send_sem=b_send.at[k, r],
-            recv_sem=b_recv.at[k, r],
+            src_ref=send_b.at[k, gg * M + mm],
+            dst_ref=recv_b.at[k, rank],
+            send_sem=b_send.at[k],
+            recv_sem=b_recv.at[k],
+            device_id=device(mm, gg),
+            device_id_type=MESH,
+        )
+
+    def b_all(k):
+        mm, gg = place(1)
+        return pltpu.make_async_remote_copy(
+            src_ref=send_b.at[k, pl.ds(0, peers - 1)],
+            dst_ref=recv_b.at[k, pl.ds(0, peers - 1)],
+            send_sem=b_send.at[k],
+            recv_sem=b_recv.at[k],
             device_id=device(mm, gg),
             device_id_type=MESH,
         )
@@ -332,8 +329,20 @@
         return pltpu.make_async_remote_copy(
             src_ref=parts.at[it, h, rows],
             dst_ref=parts.at[it, h, rows],
-            send_sem=e_send.at[it, k, r],
-            recv_sem=e_recv.at[it, k, r],
+            send_sem=e_send.at[k],
+            recv_sem=e_recv.at[it, k],
+            device_id=(hh * M + m, g),
+            device_id_type=MESH,
+        )
+
+    def e_all(it, k):
+        hh = lax.rem(h + 1, H)
+        part = parts.at[it, pl.ds(0, H - 1), pl.ds(k * PB, PB)]
+        return pltpu.make_async_remote_copy(
+            src_ref=part,
+            dst_ref=part,
+            send_sem=e_send.at[k],
+            recv_sem=e_recv.at[it, k],
             device_id=(hh * M + m, g),
             device_id_type=MESH,
         )
@@ -343,8 +352,20 @@
         return pltpu.make_async_remote_copy(
             src_ref=sums.at[it, rank],
             dst_ref=sums.at[it, rank],
-            send_sem=a_send.at[r],
-            recv_sem=a_recv.at[r],
+            send_sem=a_send.at[0],
+            recv_sem=a_recv.at[0],
+            device_id=device(mm, gg),
+            device_id_type=MESH,
+        )
+
+    def a_all(it):
+        mm, gg = place(1)
+        part = sums.at[it, pl.ds(0, peers - 1)]
+        return pltpu.make_async_remote_copy(
+            src_ref=part,
+            dst_ref=part,
+            send_sem=a_send.at[0],
+            recv_sem=a_recv.at[0],
             device_id=device(mm, gg),
             device_id_type=MESH,
         )
@@ -354,9 +375,20 @@
         return pltpu.make_async_remote_copy(
             src_ref=occ.at[m],
             dst_ref=occ.at[m],
-            send_sem=o_send.at[r],
-            recv_sem=o_recv.at[r],
+            send_sem=o_send.at[0],
+            recv_sem=o_recv.at[0],
             device_id=device(mm, g),
+            device_id_type=MESH,
+        )
+
+    def o_all():
+        part = occ.at[pl.ds(0, M - 1)]
+        return pltpu.make_async_remote_copy(
+            src_ref=part,
+            dst_ref=part,
+            send_sem=o_send.at[0],
+            recv_sem=o_recv.at[0],
+            device_id=device(lax.rem(m + 1, M), g),
             device_id_type=MESH,
         )
 
@@ -372,7 +404,7 @@
         return pltpu.make_async_remote_copy(
             src_ref=gath.at[which, m, rows],
             dst_ref=gath.at[which, m, rows],
-            send_sem=g_send.at[which, k, r],
+            send_sem=g_send.at[which],
             recv_sem=g_recv.at[which, k, r],
             device_id=device(near(r), g),
             device_id_type=MESH,
@@ -384,9 +416,30 @@
         return pltpu.make_async_remote_copy(
             src_ref=gath.at[which, block, rows],
             dst_ref=gath.at[which, block, rows],
-            send_sem=r_send.at[which, k, r],
-            recv_sem=r_recv.at[which, k, r],
+            send_sem=r_send.at[which],
+            recv_sem=r_recv.at[which],
             device_id=device(near(3 - r), g),
+            device_id_type=MESH,
+        )
+
+    def r_all(which):
+        return pltpu.make_async_remote_copy(
+            src_ref=gath.at[which, 0],
+            dst_ref=gath.at[which, 0],
+            send_sem=r_send.at[which],
+            recv_sem=r_recv.at[which],
+            device_id=device(near(1), g),
+            device_id_type=MESH,
+        )
+
+    def g_all(which):
+        part = gath.at[which, pl.ds(0, len(direct))]
+        return pltpu.make_async_remote_copy(
+            src_ref=part,
+            dst_ref=part,
+            send_sem=g_send.at[which],
+            recv_sem=g_recv.at[which, 0, 0],
+            device_id=device(near(1), g),
             device_id_type=MESH,
         )
 
@@ -403,20 +456,6 @@
     def start_all(make, count):
         def body(r, _):
             make(r).start()
-            return 0
-
-        lax.fori_loop(1, count, body, 0)
-
-    def wait_sent(make, count):
-        def body(r, _):
-            make(r).wait_send()
-            return 0
-
-        lax.fori_loop(1, count, body, 0)
-
-    def wait_arrived(make, count):
-        def body(r, _):
-            make(r).wait_recv()
             return 0
 
         lax.fori_loop(1, count, body, 0)
@@ -453,6 +492,15 @@
 
         def step(n, _):
             j = lax.rem(m + 1 + n, M)
+            if it == 0 and t == 0:
+                for tt in range(1, NB):
+                    band_load(tt, n, 0).start()
+                    band_load(tt, n, 1).start()
+
+                @pl.when(n + 1 < M)
+                def _():
+                    start_block(n + 1)
+
             if it == 0:
                 band_load(t, n, 0).wait()
                 band_load(t, n, 1).wait()
@@ -472,6 +520,9 @@
 
         if it == 0:
             lax.fori_loop(0, M, step, 0)
+            if t == 0:
+                for copy in later:
+                    copy.start()
         else:
             lax.fori_loop(0, M - 1, step, 0)
             make(m)
@@ -507,7 +558,7 @@
         def body(blk, _):
             for p in range(lowest, lowest + count):
                 v = dscr[pl.ds(blk * PL + p, C, stride=ds), :]
-                send_b[p // PB, blk // M, lax.rem(blk, M), p % PB, t] = v.astype(BF)
+                send_b[p // PB, blk, p % PB, t] = v.astype(BF)
             return 0
 
         lax.fori_loop(0, peers, body, 0)
@@ -518,7 +569,7 @@
             count = NB * M
             for n in range(count):
                 d = jnp.concatenate(
-                    [recv_b[k, n // NB, gg, pp, n % NB].astype(F32) for gg in range(G)], axis=0
+                    [recv_b[k, n // NB * G + gg, pp, n % NB].astype(F32) for gg in range(G)], axis=0
                 )
                 drhs[:kept, n * NG : (n + 1) * NG] = d.astype(BF)
                 drhs[kept:, n * NG : (n + 1) * NG] = rot(d).astype(BF)
@@ -574,7 +625,7 @@
             gsc[0] = in_lanes(kept_sums, 2 * DEPTH)
         for t in range(NB):
             with mark(f"waitF{t}"):
-                f_arrived(it, t)
+                f_all(it, t).wait_recv()
             with mark(f"X{t}"):
                 spectral(t)
             with mark(f"collect{t}"):
@@ -584,12 +635,12 @@
                     for k in range(K):
                         collect(t, k * PB, PB)
                         start_all(functools.partial(b_copy, k), peers)
-                        recv_b[k, m, g] = send_b[k, g, m]
-        if it == 0:
-            wait_arrived(o_copy, M)
+                        recv_b[k, rank] = send_b[k, own]
+        if it == 0 and M > 1:
+            o_all().wait_recv()
         for k in range(K):
             with mark(f"waitB{k}"):
-                wait_arrived(functools.partial(b_copy, k), peers)
+                b_all(k).wait_recv()
             with mark(f"C{k}"):
                 inverse_yz(it, k)
             start_all(functools.partial(e_copy, it, k), H)
@@ -597,7 +648,8 @@
         accs = tuple(jnp.zeros((8, NG), F32) for _ in range(2 * DEPTH))
         for k in range(K):
             with mark(f"waitE{k}"):
-                wait_arrived(functools.partial(e_copy, it, k), H)
+                if H > 1:
+                    e_all(it, k).wait_recv()
 
             def gather_sums(p, accs, it=it, slot=slot):
                 rho = parts[it, 0, p].astype(F32)
@@ -632,12 +684,13 @@
             for k in range(GK - 2):
                 g_pass_on(1, k)
         for t in range(NB):
-            f_sent(it, t)
+            f_all(it, t).wait_send()
         for k in range(K):
-            wait_sent(functools.partial(b_copy, k), peers)
-            wait_sent(functools.partial(e_copy, it, k), H)
+            b_all(k).wait_send()
+            if H > 1:
+                e_all(it, k).wait_send()
         with mark("waitA"):
-            wait_arrived(functools.partial(a_copy, it), peers)
+            a_all(it).wait_recv()
         total = sums[it, 0]
         for r in range(1, peers):
             total = total + sums[it, r]
@@ -669,7 +722,7 @@
                 fac[0, p] = jnp.exp(-time_step * (own + coupling * value - energy_shift))
             return 0
 
-        wait_sent(functools.partial(a_copy, it), peers)
+        a_all(it).wait_send()
         with mark("mix"):
             for k in range(GK):
                 lax.fori_loop(k * GP, (k + 1) * GP, mix, 0)
@@ -696,20 +749,20 @@
             out_copy(which, near(r)).start()
         if relay:
             with mark(f"waitR{which}"):
-                for k in range(GK):
-                    for r in direct:
-                        r_copy(which, k, r).wait_recv()
+                r_all(which).wait_recv()
             out_copy(which, 3 - m).start()
-    for which in (1, 0):
-        for block in range(M):
-            out_copy(which, block).wait()
-    wait_sent(o_copy, M)
-    for which in range(2):
-        for k in range(GK):
-            for r in direct:
-                g_copy(which, k, r).wait_send()
-                if relay:
-                    r_copy(which, k, r).wait_send()
+    with mark("outs"):
+        for which in (1, 0):
+            for block in range(M):
+                out_copy(which, block).wait()
+    with mark("drain"):
+        if M > 1:
+            o_all().wait_send()
+        for which in range(2):
+            if direct:
+                g_all(which).wait_send()
+            if relay:
+                r_all(which).wait_send()
 
 
 def widen_kernel(blocks, density, residual, density_out, residual_out, narrow, wide, in_sem, out_sem):
@@ -782,8 +835,8 @@
             pltpu.VMEM((NB, M, PL, NG, 2 * NG), BF),
             pltpu.VMEM((NB, peers, PL, C, NG), BF),
             pltpu.VMEM((NB, peers, PL, C, NG), BF),
-            pltpu.VMEM((K, G, M, PB, NB, C, NG), BF),
-            pltpu.VMEM((K, M, G, PB, NB, C, NG), BF),
+            pltpu.VMEM((K, peers, PB, NB, C, NG), BF),
+            pltpu.VMEM((K, peers, PB, NB, C, NG), BF),
             pltpu.VMEM((PL, NG, 2 * NG), BF),
             pltpu.VMEM((NG * (C + 8), NG), F32),
             pltpu.VMEM((NG, C * NG), BF),
@@ -808,20 +861,20 @@
             dma((2, M)),
             dma((NB, 2, M)),
             dma((loads,)),
-            dma((NB, peers)),
-            dma((NB, peers)),
-            dma((K, peers)),
-            dma((K, peers)),
-            dma((ITERS, K, H)),
-            dma((ITERS, K, H)),
-            dma((peers,)),
-            dma((peers,)),
-            dma((M,)),
-            dma((M,)),
+            dma((NB,)),
+            dma((NB,)),
+            dma((K,)),
+            dma((K,)),
+            dma((K,)),
+            dma((ITERS, K)),
+            dma((1,)),
+            dma((1,)),
+            dma((1,)),
+            dma((1,)),
+            dma((2,)),
             dma((2, GK, M)),
-            dma((2, GK, M)),
-            dma((2, GK, M)),
-            dma((2, GK, M)),
+            dma((2,)),
+            dma((2,)),
             dma((2, M)),
         ]
         density, residual = pl.pallas_call(

time: 157 us -> 149 us (0.949)
  Pallas kernels: 156 us -> 148 us
    pallas_call x1, Pallas kernels: 153 us -> 144 us  [local(): pl.pallas_call(functools.partial(kernel, dims), in_specs=[smem] + [hbm] *...]
where the time goes in v4:
time: 149 us; the launch traced here: 148 us
  Pallas kernels  148 us (99%)
    pallas_call x1, Pallas kernels, local(): pl.pallas_call(functools.partial(kernel, dims), in_specs=[smem] + [hbm] *...  144 us
    pallas_call x1, Pallas kernels, widen(): pl.pallas_call(functools.partial(widen_kernel, blocks), in_specs=[hbm] *...  3.12 us

profile of v4, /device:TPU:0, one launch (start us, length us, event | category | flops | bytes accessed | tf_op | source)
XLA Modules:
  0.0 148.4 jit_solution(6586575033439930546)
XLA Ops:
  0.6 144.5 %scf.1 = (bf16[32,128,128]{2,1,0:T(8,128)(2,1)}, bf16[32,128,128]{2,1,0:T(8,128)(2,1)}) custom-call(f32[2]{0:T(128)} %occ_in.1, bf16[2,2,32,128,128]{4,3,2,1,0:T(8,128)(2,1)} %bands.1, f32[32,128,128]{2,1,0:T(8,128)} %external.1, f32[32,128,128]{2,1,0:T(8,128)} %density_in.1, f32[32,128,128]{2,1,0:T(8,128)} %prev_density.1, f32[32,128,128]{2,1,0:T(8,128)} %prev_residual.1, ...), custom_call_target="tpu_custom_call" | custom-call | tf_op jit(solution)/shard_map/scf/pallas_call | solution.py:880
  145.1 3.1 %widen.1 = (f32[32,128,128]{2,1,0:T(8,128)}, f32[32,128,128]{2,1,0:T(8,128)}) custom-call(bf16[32,128,128]{2,1,0:T(8,128)(2,1)} %get-tuple-element.4.density, bf16[32,128,128]{2,1,0:T(8,128)(2,1)} %get-tuple-element.5.residual), custom_call_target="tpu_custom_call" | custom-call | tf_op jit(solution)/shard_map/widen/pallas_call | solution.py:787

commit v5 on v4

--- a/solution.py
+++ b/solution.py
@@ -182,16 +182,30 @@
     h = b // M
     rank = m * G + g
 
+    paired = M == 4 and G == 4
+
+    def across(a, v):
+        high, low, vh, vl = a // 2, lax.rem(a, 2), v // 2, v % 2
+        return 2 * (high + vh - 2 * high * vh) + low + vl - 2 * low * vl
+
+    def block_at(n):
+        return across(m, M - 1 - n) if paired else lax.rem(m + 1 + n, M)
+
+    def lane_at(r):
+        return across(g, G - r) if paired else lax.rem(g + r, G)
+
     def place(r):
+        if paired:
+            v = peers - r
+            return across(m, v // G), across(g, v % G)
         other = lax.rem(rank + r, peers)
         return other // G, lax.rem(other, G)
 
-    def source(r):
-        other = lax.rem(rank + peers - r, peers)
-        return other // G, lax.rem(other, G)
-
     def device(mm, gg):
         return (h * M + mm, gg)
+
+    places = [None] + [place(r) for r in range(1, peers)]
+    lanes = [None] + [lane_at(r) for r in range(1, G)] + [g]
 
     loads = []
 
@@ -216,12 +230,12 @@
     ]
 
     def field_load(n, i):
-        block = pl.ds(lax.rem(m + 1 + n, M) * PL, PL)
+        block = pl.ds(block_at(n) * PL, PL)
         src, dst = ((external, ext), (density_in, rho0))[i]
         return pltpu.make_async_copy(src.at[block], dst.at[block], field_sem.at[i, n])
 
     def band_load(t, n, c):
-        j = lax.rem(m + 1 + n, M)
+        j = block_at(n)
         return pltpu.make_async_copy(
             bands.at[c, t, pl.ds(j * PL, PL)],
             psi.at[t, j, :, :, pl.ds(c * NG, NG)],
@@ -236,7 +250,8 @@
 
     for copy in tables:
         copy.start()
-    start_block(0)
+    for n in range(min(2, M)):
+        start_block(n)
     mine = pl.ds(m * PL, PL)
     later = [
         load(density_in.at[mine], now.at[0]),
@@ -291,7 +306,7 @@
 
     def f_all(it, t):
         blocks = pl.ds(0, peers - M if it == 0 else peers - 1)
-        mm, gg = place(1)
+        mm, gg = places[1]
         return pltpu.make_async_remote_copy(
             src_ref=send_f.at[t, blocks],
             dst_ref=recv_f.at[t, blocks],
@@ -313,7 +328,7 @@
         )
 
     def b_all(k):
-        mm, gg = place(1)
+        mm, gg = places[1]
         return pltpu.make_async_remote_copy(
             src_ref=send_b.at[k, pl.ds(0, peers - 1)],
             dst_ref=recv_b.at[k, pl.ds(0, peers - 1)],
@@ -348,7 +363,7 @@
         )
 
     def a_copy(it, r):
-        mm, gg = place(r)
+        mm, gg = places[r]
         return pltpu.make_async_remote_copy(
             src_ref=sums.at[it, rank],
             dst_ref=sums.at[it, rank],
@@ -359,7 +374,7 @@
         )
 
     def a_all(it):
-        mm, gg = place(1)
+        mm, gg = places[1]
         part = sums.at[it, pl.ds(0, peers - 1)]
         return pltpu.make_async_remote_copy(
             src_ref=part,
@@ -405,7 +420,7 @@
             src_ref=gath.at[which, m, rows],
             dst_ref=gath.at[which, m, rows],
             send_sem=g_send.at[which],
-            recv_sem=g_recv.at[which, k, r],
+            recv_sem=g_recv.at[which, k, r - 1],
             device_id=device(near(r), g),
             device_id_type=MESH,
         )
@@ -454,6 +469,10 @@
                 r_copy(which, k, r).start()
 
     def start_all(make, count):
+        for r in range(1, count):
+            make(r).start()
+
+    def start_paced(make, count):
         def body(r, _):
             make(r).start()
             return 0
@@ -479,27 +498,27 @@
                             gg * C : (gg + 1) * C, side * NG : (side + 1) * NG
                         ]
 
-        def send(j, lowest):
-            def body(r, _):
-                gg = lax.rem(g + r, G)
+        def send(j, upper):
+            for r in range(1, upper):
+                gg = lanes[r]
                 if it == 0:
                     f_copy(t, gg, j, g * M + j, m).start()
                 else:
                     f_copy(t, gg, j, own, j).start()
-                return 0
-
-            lax.fori_loop(lowest, G, body, 0)
 
         def step(n, _):
-            j = lax.rem(m + 1 + n, M)
+            j = block_at(n)
             if it == 0 and t == 0:
-                for tt in range(1, NB):
-                    band_load(tt, n, 0).start()
-                    band_load(tt, n, 1).start()
-
-                @pl.when(n + 1 < M)
+
+                @pl.when(n + 2 < M)
                 def _():
-                    start_block(n + 1)
+                    start_block(n + 2)
+
+                @pl.when(n > 0)
+                def _():
+                    for tt in range(1, NB):
+                        band_load(tt, n - 1, 0).start()
+                        band_load(tt, n - 1, 1).start()
 
             if it == 0:
                 band_load(t, n, 0).wait()
@@ -513,7 +532,7 @@
                         -time_step * (ext[plane] + coupling * rho0[plane] - energy_shift)
                     )
             make(j)
-            send(j, 1 if it == 0 else 0)
+            send(j, G if it == 0 else G + 1)
             if it == 0:
                 recv_f[t, g * M + j] = send_f[t, g * M + j]
             return 0
@@ -521,12 +540,15 @@
         if it == 0:
             lax.fori_loop(0, M, step, 0)
             if t == 0:
+                for tt in range(1, NB):
+                    band_load(tt, M - 1, 0).start()
+                    band_load(tt, M - 1, 1).start()
                 for copy in later:
                     copy.start()
         else:
             lax.fori_loop(0, M - 1, step, 0)
             make(m)
-            send(m, 1)
+            send(m, G)
             recv_f[t, own] = send_f[t, own]
 
     def spectral(t):
@@ -634,7 +656,7 @@
                 else:
                     for k in range(K):
                         collect(t, k * PB, PB)
-                        start_all(functools.partial(b_copy, k), peers)
+                        start_paced(functools.partial(b_copy, k), peers)
                         recv_b[k, rank] = send_b[k, own]
         if it == 0 and M > 1:
             o_all().wait_recv()
@@ -872,7 +894,7 @@
             dma((1,)),
             dma((1,)),
             dma((2,)),
-            dma((2, GK, M)),
+            dma((2, GK, 2 if M == 4 else max(1, M - 1))),
             dma((2,)),
             dma((2,)),
             dma((2, M)),

time: 149 us -> 147 us (0.987)
  Pallas kernels: 148 us -> 146 us
    pallas_call x1, Pallas kernels: 144 us -> 142 us  [local(): pl.pallas_call(functools.partial(kernel, dims), in_specs=[smem] + [hbm] *...]
where the time goes in v5:
time: 147 us; the launch traced here: 146 us
  Pallas kernels  146 us (99%)
    pallas_call x1, Pallas kernels, local(): pl.pallas_call(functools.partial(kernel, dims), in_specs=[smem] + [hbm] *...  142 us
    pallas_call x1, Pallas kernels, widen(): pl.pallas_call(functools.partial(widen_kernel, blocks), in_specs=[hbm] *...  3.12 us

profile of v5, /device:TPU:0, one launch (start us, length us, event | category | flops | bytes accessed | tf_op | source)
XLA Modules:
  0.0 146.4 jit_solution(3268175820899504531)
XLA Ops:
  0.6 142.5 %scf.1 = (bf16[32,128,128]{2,1,0:T(8,128)(2,1)}, bf16[32,128,128]{2,1,0:T(8,128)(2,1)}) custom-call(f32[2]{0:T(128)} %occ_in.1, bf16[2,2,32,128,128]{4,3,2,1,0:T(8,128)(2,1)} %bands.1, f32[32,128,128]{2,1,0:T(8,128)} %external.1, f32[32,128,128]{2,1,0:T(8,128)} %density_in.1, f32[32,128,128]{2,1,0:T(8,128)} %prev_density.1, f32[32,128,128]{2,1,0:T(8,128)} %prev_residual.1, ...), custom_call_target="tpu_custom_call" | custom-call | tf_op jit(solution)/shard_map/scf/pallas_call | solution.py:902
  143.1 3.1 %widen.1 = (f32[32,128,128]{2,1,0:T(8,128)}, f32[32,128,128]{2,1,0:T(8,128)}) custom-call(bf16[32,128,128]{2,1,0:T(8,128)(2,1)} %get-tuple-element.4.density, bf16[32,128,128]{2,1,0:T(8,128)(2,1)} %get-tuple-element.5.residual), custom_call_target="tpu_custom_call" | custom-call | tf_op jit(solution)/shard_map/widen/pallas_call | solution.py:809
